TPU v7x, 32 devices: a whole 2x2x4 slice. The times are simulated.
32 devices in a mesh: dp: 2 (over x), tp: 16 (over z, y, core).
Axes of the slice: x: 2, y: 2, z: 4, core: 2. Of those that a mesh axis runs over, the one named last changes fastest.
Arguments:
- token_ids: int32 [2, 256], P('dp'), parts along dimension 0
- embed_table: bfloat16 [8192, 4096], P('tp')
- emb_gain: float32 [4096], replicated
- emb_bias: float32 [4096], replicated
- ln1_gain: float32 [4096], replicated
- ln1_bias: float32 [4096], replicated
- w_qkv: bfloat16 [4096, 32, 3, 128], P(None, 'tp')
- b_qkv: float32 [32, 3, 128], P('tp')
- w_dense: bfloat16 [4096, 4096], P('tp')
- b_dense: float32 [4096], replicated
- ln2_gain: float32 [4096], replicated
- ln2_bias: float32 [4096], replicated
- w_fc1: bfloat16 [4096, 16384], P(None, 'tp')
- b_fc1: float32 [16384], P('tp')
- w_fc2: bfloat16 [16384, 4096], P('tp')
- b_fc2: float32 [4096], replicated
- d_out: bfloat16 [2, 256, 4096], P('dp', 'tp'), parts along dimension 0
Outputs:
- output 1: bfloat16 [2, 256, 4096], P('dp', 'tp'), parts along dimension 0
- output 2: float32 [16384, 4096], P(('dp', 'tp')), parts along dimension 0
- output 3: float32 [8192], P('dp'), parts along dimension 0
- output 4: float32 [8192], P('dp'), parts along dimension 0
- output 5: float32 [8192], P('dp'), parts along dimension 0
- output 6: float32 [8192], P('dp'), parts along dimension 0
- output 7: bfloat16 [8192, 32, 3, 128], P('dp', 'tp'), parts along dimension 0
- output 8: float32 [64, 3, 128], P(('dp', 'tp')), parts along dimension 0
- output 9: bfloat16 [8192, 4096], P(('dp', 'tp')), parts along dimension 0
- output 10: float32 [8192], P('dp'), parts along dimension 0
- output 11: float32 [8192], P('dp'), parts along dimension 0
- output 12: float32 [8192], P('dp'), parts along dimension 0
- output 13: bfloat16 [8192, 16384], P('dp', 'tp'), parts along dimension 0
- output 14: float32 [32768], P(('dp', 'tp')), parts along dimension 0
- output 15: bfloat16 [32768, 4096], P(('dp', 'tp')), parts along dimension 0
- output 16: float32 [8192], P('dp'), parts along dimension 0
There are 2 independent parts. A program takes and returns all parts, laid end to end along the dimension named above; an argument that names none is the same for every part.
All inputs are finite; a program needn't handle non-finite values.
Results may differ from a plain program's by a relative error of at most 0.02.
Values are sent between devices in bfloat16 or wider.
A program may use at most 1 GiB of HBM per device.

v0:
```python
import functools
import jax
import jax.numpy as jnp
from jax import lax
from jax.sharding import PartitionSpec as P

EPS = 1e-5


def alibi_slopes(head_count):
    closest = 2 ** (head_count.bit_length() - 1)
    slope_base = 2.0 ** (-8.0 / closest)
    extra_base = 2.0 ** (-4.0 / closest)
    slopes = [slope_base ** exponent for exponent in range(1, closest + 1)]
    slopes = slopes + [extra_base ** exponent for exponent in range(1, 2 * (head_count - closest), 2)]
    return jnp.array(slopes, dtype=jnp.float32)


def norm_forward(values, gain_vec, bias_vec):
    centered = values - jnp.mean(values, axis=-1, keepdims=True)
    inv_std = lax.rsqrt(jnp.mean(centered * centered, axis=-1, keepdims=True) + EPS)
    x_hat = centered * inv_std
    return x_hat * gain_vec + bias_vec, x_hat, inv_std


def norm_backward(d_norm, x_hat, inv_std, gain_vec):
    d_hat = d_norm * gain_vec
    d_values = inv_std * (d_hat - jnp.mean(d_hat, axis=-1, keepdims=True)
                          - x_hat * jnp.mean(d_hat * x_hat, axis=-1, keepdims=True))
    return d_values, jnp.sum(d_norm * x_hat, axis=(0, 1)), jnp.sum(d_norm, axis=(0, 1))


def device_step(token_ids, embed_table, emb_gain, emb_bias, ln1_gain, ln1_bias,
                w_qkv, b_qkv, w_dense, b_dense, ln2_gain, ln2_bias,
                w_fc1, b_fc1, w_fc2, b_fc2, d_out, slopes_all):
    tp_index = lax.axis_index('tp')
    batch_size, seq_len = token_ids.shape
    vocab_rows = embed_table.shape[0]
    local_heads, head_dim = w_qkv.shape[1], w_qkv.shape[3]
    attn_scale = head_dim ** -0.5

    local_ids = token_ids - tp_index * vocab_rows
    in_range = (local_ids >= 0) & (local_ids < vocab_rows)
    table_rows = jnp.take(embed_table, jnp.clip(local_ids, 0, vocab_rows - 1), axis=0)
    emb_part = jnp.where(in_range[:, :, None], table_rows, jnp.zeros((), jnp.bfloat16))
    emb_sum = lax.psum_scatter(emb_part, 'tp', scatter_dimension=1, tiled=True)

    e_norm, e_hat, e_inv = norm_forward(emb_sum.astype(jnp.float32), emb_gain, emb_bias)
    embedded = e_norm.astype(jnp.bfloat16)
    n1_norm, n1_hat, n1_inv = norm_forward(embedded.astype(jnp.float32), ln1_gain, ln1_bias)
    h_one_full = lax.all_gather(n1_norm.astype(jnp.bfloat16), 'tp', axis=1, tiled=True)
    qkv_all = (jnp.einsum('bsd,dhce->bshce', h_one_full, w_qkv, preferred_element_type=jnp.float32) + b_qkv).astype(jnp.bfloat16)
    q_part, k_part, v_part = qkv_all[:, :, :, 0], qkv_all[:, :, :, 1], qkv_all[:, :, :, 2]

    slopes = lax.dynamic_slice_in_dim(slopes_all, tp_index * local_heads, local_heads)
    positions = jnp.arange(seq_len)
    rel_pos = (positions[None, :] - positions[:, None]).astype(jnp.float32)
    causal = positions[None, :] <= positions[:, None]
    scores = jnp.einsum('bqhe,bkhe->bhqk', q_part, k_part, preferred_element_type=jnp.float32) * attn_scale
    scores = jnp.where(causal, scores + slopes[:, None, None] * rel_pos, -1e30)
    prob_f32 = jax.nn.softmax(scores, axis=-1)
    prob_bf = prob_f32.astype(jnp.bfloat16)
    context = jnp.einsum('bhqk,bkhe->bqhe', prob_bf, v_part, preferred_element_type=jnp.float32).astype(jnp.bfloat16)
    context = context.reshape(batch_size, seq_len, local_heads * head_dim)

    dense_part = jnp.einsum('bsc,cd->bsd', context, w_dense, preferred_element_type=jnp.float32).astype(jnp.bfloat16)
    dense_sum = lax.psum_scatter(dense_part, 'tp', scatter_dimension=1, tiled=True)
    r_one = (embedded.astype(jnp.float32) + dense_sum.astype(jnp.float32) + b_dense).astype(jnp.bfloat16)
    n2_norm, n2_hat, n2_inv = norm_forward(r_one.astype(jnp.float32), ln2_gain, ln2_bias)
    h_two_full = lax.all_gather(n2_norm.astype(jnp.bfloat16), 'tp', axis=1, tiled=True)
    pre_act = jnp.einsum('bsd,df->bsf', h_two_full, w_fc1, preferred_element_type=jnp.float32) + b_fc1
    gelu_out, gelu_pull = jax.vjp(functools.partial(jax.nn.gelu, approximate=True), pre_act)
    gelu_bf = gelu_out.astype(jnp.bfloat16)
    mlp_part = jnp.einsum('bsf,fd->bsd', gelu_bf, w_fc2, preferred_element_type=jnp.float32).astype(jnp.bfloat16)
    mlp_sum = lax.psum_scatter(mlp_part, 'tp', scatter_dimension=1, tiled=True)
    y_out = (r_one.astype(jnp.float32) + mlp_sum.astype(jnp.float32) + b_fc2).astype(jnp.bfloat16)

    dy_f32 = d_out.astype(jnp.float32)
    dy_full = lax.all_gather(d_out, 'tp', axis=1, tiled=True)
    d_w_fc2 = jnp.einsum('bsf,bsd->fd', gelu_bf, dy_full, preferred_element_type=jnp.float32).astype(jnp.bfloat16)
    d_gelu = jnp.einsum('bsd,fd->bsf', dy_full, w_fc2, preferred_element_type=jnp.float32)
    (d_pre,) = gelu_pull(d_gelu)
    d_pre_bf = d_pre.astype(jnp.bfloat16)
    d_b_fc1 = jnp.sum(d_pre, axis=(0, 1))
    d_w_fc1 = jnp.einsum('bsd,bsf->df', h_two_full, d_pre_bf, preferred_element_type=jnp.float32).astype(jnp.bfloat16)
    dh2_part = jnp.einsum('bsf,df->bsd', d_pre_bf, w_fc1, preferred_element_type=jnp.float32).astype(jnp.bfloat16)
    dh2_sum = lax.psum_scatter(dh2_part, 'tp', scatter_dimension=1, tiled=True)
    dr1_norm, d_ln2_gain, d_ln2_bias = norm_backward(dh2_sum.astype(jnp.float32), n2_hat, n2_inv, ln2_gain)
    dr1_f32 = dy_f32 + dr1_norm
    dr1_full = lax.all_gather(dr1_f32.astype(jnp.bfloat16), 'tp', axis=1, tiled=True)
    d_w_dense = jnp.einsum('bsc,bsd->cd', context, dr1_full, preferred_element_type=jnp.float32).astype(jnp.bfloat16)
    d_context = jnp.einsum('bsd,cd->bsc', dr1_full, w_dense, preferred_element_type=jnp.float32).astype(jnp.bfloat16)
    d_context = d_context.reshape(batch_size, seq_len, local_heads, head_dim)

    d_value = jnp.einsum('bhqk,bqhe->bkhe', prob_bf, d_context, preferred_element_type=jnp.float32)
    d_prob = jnp.einsum('bqhe,bkhe->bhqk', d_context, v_part, preferred_element_type=jnp.float32)
    d_score = prob_f32 * (d_prob - jnp.sum(d_prob * prob_f32, axis=-1, keepdims=True))
    d_score_bf = (d_score * attn_scale).astype(jnp.bfloat16)
    d_query = jnp.einsum('bhqk,bkhe->bqhe', d_score_bf, k_part, preferred_element_type=jnp.float32)
    d_key = jnp.einsum('bhqk,bqhe->bkhe', d_score_bf, q_part, preferred_element_type=jnp.float32)
    d_qkv = jnp.stack([d_query, d_key, d_value], axis=3)
    d_b_qkv = jnp.sum(d_qkv, axis=(0, 1))
    d_qkv_bf = d_qkv.astype(jnp.bfloat16)
    d_w_qkv = jnp.einsum('bsd,bshce->dhce', h_one_full, d_qkv_bf, preferred_element_type=jnp.float32).astype(jnp.bfloat16)
    dh1_part = jnp.einsum('bshce,dhce->bsd', d_qkv_bf, w_qkv, preferred_element_type=jnp.float32).astype(jnp.bfloat16)
    dh1_sum = lax.psum_scatter(dh1_part, 'tp', scatter_dimension=1, tiled=True)
    de_norm, d_ln1_gain, d_ln1_bias = norm_backward(dh1_sum.astype(jnp.float32), n1_hat, n1_inv, ln1_gain)
    dx_norm, d_emb_gain, d_emb_bias = norm_backward(dr1_f32 + de_norm, e_hat, e_inv, emb_gain)
    dx_full = lax.all_gather(dx_norm.astype(jnp.bfloat16), 'tp', axis=1, tiled=True)
    one_hot = (local_ids[:, :, None] == jnp.arange(vocab_rows)).astype(jnp.bfloat16)
    d_table = jnp.einsum('bsv,bsd->vd', one_hot, dx_full, preferred_element_type=jnp.float32)

    small_sums = lax.psum((d_emb_gain, d_emb_bias, d_ln1_gain, d_ln1_bias, jnp.sum(dr1_f32, axis=(0, 1)),
                           d_ln2_gain, d_ln2_bias, jnp.sum(dy_f32, axis=(0, 1))), 'tp')
    return (y_out, d_table, small_sums[0], small_sums[1], small_sums[2], small_sums[3],
            d_w_qkv, d_b_qkv, d_w_dense, small_sums[4], small_sums[5], small_sums[6],
            d_w_fc1, d_b_fc1, d_w_fc2, small_sums[7])


def solution(mesh):
    in_specs = (P('dp', None), P('tp', None), P(None), P(None), P(None), P(None),
                P(None, 'tp', None, None), P('tp', None, None), P('tp', None), P(None),
                P(None), P(None), P(None, 'tp'), P('tp'), P('tp', None), P(None),
                P('dp', 'tp', None), P(None))
    out_specs = (P('dp', 'tp', None), P(('dp', 'tp'), None), P('dp'), P('dp'), P('dp'), P('dp'),
                 P('dp', 'tp', None, None), P(('dp', 'tp'), None, None), P(('dp', 'tp'), None), P('dp'),
                 P('dp'), P('dp'), P('dp', 'tp'), P(('dp', 'tp')), P(('dp', 'tp'), None), P('dp'))
    mapped = jax.shard_map(device_step, mesh=mesh, in_specs=in_specs, out_specs=out_specs, check_vma=False)

    def run(*arrays):
        slopes_all = alibi_slopes(arrays[6].shape[1])
        return mapped(*arrays, slopes_all)

    return run
```

profile of v0, /device:TPU:0, one launch (start us, length us, event | category | flops | bytes accessed | tf_op | source)
XLA Modules:
  0.0 734.2 jit_solution(9100336425918448973)
XLA Ops:
  8.7 7.9 %gather_fusion = bf16[256,4096]{1,0:T(8,128)(2,1)} fusion(bf16[512,4096]{1,0:T(8,128)(2,1)} %param.19, s32[1024]{0:T(1024)S(1)} %pad_clamp_fusion), kind=kCustom, calls=%fused_computation | custom fusion | bytes 4195328 | tf_op jit(solution)/shard_map/jit(_take)/gather | solution.py:44
  16.6 3.2 fusion.31
  19.9 64.6 %reduce-scatter.6.cloned.1.call-done = bf16[1,16,4096]{2,1,0:T(8,128)(2,1)} async-done(((bf16[1,256,4096]{2,1,0:T(8,128)(2,1)}), bf16[1,16,4096]{2,1,0:T(8,128)(2,1)}) %reduce-scatter.6.cloned.1.call-update) | async-done | bytes 131088 | tf_op jit(solution)/shard_map/reduce_scatter | solution.py:46
  89.3 40.6 %all-gather.6.cloned.1.call-done = bf16[1,256,4096]{2,1,0:T(8,128)(2,1)} async-done(((bf16[1,16,4096]{2,1,0:T(8,128)(2,1)}), bf16[1,256,4096]{2,1,0:T(8,128)(2,1)}) %all-gather.6.cloned.1.call-update) | async-done | bytes 2097168 | tf_op jit(solution)/shard_map/all_gather | solution.py:51
  129.9 5.2 fusion.52
  137.5 2.1 fusion.15
  139.6 60.4 %reduce-scatter.8.cloned.1.call-done = bf16[1,16,4096]{2,1,0:T(8,128)(2,1)} async-done(((bf16[1,256,4096]{2,1,0:T(8,128)(2,1)}), bf16[1,16,4096]{2,1,0:T(8,128)(2,1)}) %reduce-scatter.8.cloned.1.call-update) | async-done | bytes 131088 | tf_op jit(solution)/shard_map/reduce_scatter | solution.py:67
  203.0 40.4 %all-gather.8.cloned.1.call-done = bf16[1,256,4096]{2,1,0:T(8,128)(2,1)} async-done(((bf16[1,16,4096]{2,1,0:T(8,128)(2,1)}), bf16[1,256,4096]{2,1,0:T(8,128)(2,1)}) %all-gather.8.cloned.1.call-update) | async-done | bytes 2097168 | tf_op jit(solution)/shard_map/all_gather | solution.py:70
  243.4 7.3 fusion.32
  250.7 35.0 %all-gather.10.cloned.1.call-done = bf16[1,256,4096]{2,1,0:T(8,128)(2,1)} async-done(((bf16[1,16,4096]{2,1,0:T(8,128)(2,1)}), bf16[1,256,4096]{2,1,0:T(8,128)(2,1)}) %all-gather.10.cloned.1.call-update) | async-done | bytes 2097168 | tf_op jit(solution)/shard_map/all_gather | solution.py:79
  285.6 7.7 %fusion.146 = (f32[1024]{0:T(1024)}, bf16[256,1024]{1,0:T(8,128)(2,1)S(1)}) fusion(f32[256,1024]{1,0:T(8,128)} %fusion.32, bf16[1024,4096]{1,0:T(8,128)(2,1)} %param.32, bf16[1,256,4096]{2,1,0:T(8,128)(2,1)} %all-gather.10.cloned.1.call-done), kind=kOutput, calls=%fused_computation.177 | convolution fusion | flops 2152987648 | bytes 12062720 | tf_op jit(solution)/shard_map/bsd,fd->bsf/dot_general | solution.py:81
  294.2 7.1 fusion.17
  301.3 7.5 %fusion.16 = bf16[1,256,4096]{2,1,0:T(8,128)(2,1)} fusion(bf16[1024,4096]{1,0:T(8,128)(2,1)} %param.32, f32[256,1024]{1,0:T(8,128)} %fusion.32), kind=kOutput, calls=%fused_computation.18 | convolution fusion | flops 2150891520 | bytes 11534336 | tf_op jit(solution)/shard_map/bsf,fd->bsd/dot_general | solution.py:74
  308.9 52.8 %reduce-scatter.12.cloned.1.call-done = bf16[1,16,4096]{2,1,0:T(8,128)(2,1)} async-done(((bf16[1,256,4096]{2,1,0:T(8,128)(2,1)}), bf16[1,16,4096]{2,1,0:T(8,128)(2,1)}) %reduce-scatter.12.cloned.1.call-update) | async-done | bytes 131088 | tf_op jit(solution)/shard_map/reduce_scatter | solution.py:87
  361.7 1.7 fusion.123
  363.4 63.4 %reduce-scatter.10.cloned.1.call-done = bf16[1,16,4096]{2,1,0:T(8,128)(2,1)} async-done(((bf16[1,256,4096]{2,1,0:T(8,128)(2,1)}), bf16[1,16,4096]{2,1,0:T(8,128)(2,1)}) %reduce-scatter.10.cloned.1.call-update) | async-done | bytes 131088 | tf_op jit(solution)/shard_map/reduce_scatter | solution.py:75
  426.8 2.4 fusion.141
  430.2 40.6 %all-gather.12.cloned.1.call-done = bf16[1,256,4096]{2,1,0:T(8,128)(2,1)} async-done(((bf16[1,16,4096]{2,1,0:T(8,128)(2,1)}), bf16[1,256,4096]{2,1,0:T(8,128)(2,1)}) %all-gather.12.cloned.1.call-update) | async-done | bytes 2097168 | tf_op jit(solution)/shard_map/all_gather | solution.py:90
  470.7 2.3 fusion.58
  474.4 1.5 fusion.62
  475.9 1.5 fusion.61
  478.8 6.0 fusion.12
  484.8 60.4 %reduce-scatter.14.cloned.1.call-done = bf16[1,16,4096]{2,1,0:T(8,128)(2,1)} async-done(((bf16[1,256,4096]{2,1,0:T(8,128)(2,1)}), bf16[1,16,4096]{2,1,0:T(8,128)(2,1)}) %reduce-scatter.14.cloned.1.call-update) | async-done | bytes 131088 | tf_op jit(solution)/shard_map/reduce_scatter | solution.py:106
  545.2 1.7 fusion.124
  546.9 1.8 fusion.115
  550.4 7.0 convolution_convert_fusion.1
  557.4 6.0 convolution_convert_fusion
  563.4 2.9 convolution_convert_fusion.2
  566.3 56.0 %copy.63 = bf16[4096,2,3,128]{3,1,2,0:T(2,128)(2,1)} copy(bf16[4096,2,3,128]{3,0,2,1:T(8,128)(2,1)S(1)} %convolution_convert_fusion.2) | data formatting | bytes 12582912
  623.1 2.0 convolution_convert_fusion.5
  625.2 6.5 fusion.20
  631.7 85.4 %all-reduce.3.cloned.1.call-done = (f32[4096]{0:T(1024)}, f32[4096]{0:T(1024)}, f32[4096]{0:T(1024)}, f32[4096]{0:T(1024)}, f32[4096]{0:T(1024)}, /*index=5*/f32[4096]{0:T(1024)}, f32[4096]{0:T(1024)}, f32[4096]{0:T(1024)}) async-done(((f32[4096]{0:T(1024)}, f32[4096]{0:T(1024)}, f32[4096]{0:T(1024)}, f32[4096]{0:T(1024)}, f32[4096]{0:T(1024)}, /*index=5*/f32[4096]{0:T(1024)}, f32[4096]{0:T(1024)}, ...) | async-done | bytes 131088 | tf_op jit(solution)/shard_map/psum | solution.py:113
  (142 shorter events, 28.9 us)
Async XLA Ops:
  7.2 130.3 %copy-start = (bf16[256,4096]{1,0:T(8,128)(2,1)S(1)}, bf16[256,4096]{1,0:T(8,128)(2,1)}, u32[]{:S(2)}) copy-start(bf16[256,4096]{1,0:T(8,128)(2,1)} %param.26) | copy-start | bytes 6291460
  7.2 77.4 %reduce-scatter.6.cloned.1.call-start = ((), (), s32[]{:S(2)}) async-start(), calls=%async_computation.5 | async-start | bytes 2228224 | tf_op jit(solution)/shard_map/reduce_scatter | solution.py:46
  19.8 66.9 %copy-start.13 = (f32[4096]{0:T(1024)S(1)}, f32[4096]{0:T(1024)}, u32[]{:S(2)}) copy-start(f32[4096]{0:T(1024)} %param.20) | copy-start | bytes 49156
  19.8 66.9 %copy-start.23 = (f32[4096]{0:T(1024)S(1)}, f32[4096]{0:T(1024)}, u32[]{:S(2)}) copy-start(f32[4096]{0:T(1024)} %param.21) | copy-start | bytes 49156
  19.8 68.4 %copy-start.12 = (f32[4096]{0:T(1024)S(1)}, f32[4096]{0:T(1024)}, u32[]{:S(2)}) copy-start(f32[4096]{0:T(1024)} %param.22) | copy-start | bytes 49156
  19.8 68.4 %copy-start.24 = (f32[4096]{0:T(1024)S(1)}, f32[4096]{0:T(1024)}, u32[]{:S(2)}) copy-start(f32[4096]{0:T(1024)} %param.23) | copy-start | bytes 49156
  19.8 69.2 %copy-start.31 = (f32[2,3,128]{2,0,1:T(2,128)S(1)}, f32[2,3,128]{2,0,1:T(2,128)}, u32[]{:S(2)}) copy-start(f32[2,3,128]{2,0,1:T(2,128)} %param.25) | copy-start | bytes 9220
  19.9 69.2 %copy-start.36 = (f32[32]{0:T(128)S(1)}, f32[32]{0:T(128)}, u32[]{:S(2)}) copy-start(f32[32]{0:T(128)} %constant.70.clone) | copy-start | bytes 388
  19.9 110.0 %all-gather.6.cloned.1.call-start = ((), (), s32[]{:S(2)}) async-start(), calls=%async_computation.6 | async-start | bytes 2228224 | tf_op jit(solution)/shard_map/all_gather | solution.py:51
  89.0 111.0 %reduce-scatter.8.cloned.1.call-start = ((), (), s32[]{:S(2)}) async-start(), calls=%async_computation.7 | async-start | bytes 2228224 | tf_op jit(solution)/shard_map/reduce_scatter | solution.py:67
  139.5 60.5 %copy-start.25 = (f32[4096]{0:T(1024)S(1)}, f32[4096]{0:T(1024)}, u32[]{:S(2)}) copy-start(f32[4096]{0:T(1024)} %param.27) | copy-start | bytes 49156
  139.6 61.8 %copy-start.11 = (f32[4096]{0:T(1024)S(1)}, f32[4096]{0:T(1024)}, u32[]{:S(2)}) copy-start(f32[4096]{0:T(1024)} %param.28) | copy-start | bytes 49156
  139.6 61.8 %copy-start.26 = (f32[4096]{0:T(1024)S(1)}, f32[4096]{0:T(1024)}, u32[]{:S(2)}) copy-start(f32[4096]{0:T(1024)} %param.29) | copy-start | bytes 49156
  139.6 103.8 %copy-start.35 = (f32[1024]{0:T(1024)S(1)}, f32[1024]{0:T(1024)}, u32[]{:S(2)}) copy-start(f32[1024]{0:T(1024)} %param.31) | copy-start | bytes 12292
  139.6 103.8 %all-gather.8.cloned.1.call-start = ((), (), s32[]{:S(2)}) async-start(), calls=%async_computation.8 | async-start | bytes 2228224 | tf_op jit(solution)/shard_map/all_gather | solution.py:70
  202.2 83.5 %all-gather.10.cloned.1.call-start = ((), (), s32[]{:S(2)}) async-start(), calls=%async_computation.10 | async-start | bytes 2228224 | tf_op jit(solution)/shard_map/all_gather | solution.py:79
  202.7 159.0 %reduce-scatter.12.cloned.1.call-start = ((), (), s32[]{:S(2)}) async-start(), calls=%async_computation.11 | async-start | bytes 2228224 | tf_op jit(solution)/shard_map/reduce_scatter | solution.py:87
  301.3 125.6 %reduce-scatter.10.cloned.1.call-start = ((), (), s32[]{:S(2)}) async-start(), calls=%async_computation.9 | async-start | bytes 2228224 | tf_op jit(solution)/shard_map/reduce_scatter | solution.py:75
  308.8 118.0 %copy-start.8 = (bf16[1,16,4096]{2,1,0:T(8,128)(2,1)S(1)}, bf16[1,16,4096]{2,1,0:T(8,128)(2,1)}, u32[]{:S(2)}) copy-start(bf16[1,16,4096]{2,1,0:T(8,128)(2,1)} %param.34) | copy-start | bytes 393220
  308.8 118.0 %copy-start.22 = (f32[4096]{0:T(1024)S(1)}, f32[4096]{0:T(1024)}, u32[]{:S(2)}) copy-start(f32[4096]{0:T(1024)} %param.33) | copy-start | bytes 49156
  308.8 161.9 %all-gather.12.cloned.1.call-start = ((), (), s32[]{:S(2)}) async-start(), calls=%async_computation.12 | async-start | bytes 2228224 | tf_op jit(solution)/shard_map/all_gather | solution.py:90
  429.9 115.3 %reduce-scatter.14.cloned.1.call-start = ((), (), s32[]{:S(2)}) async-start(), calls=%async_computation.13 | async-start | bytes 2228224 | tf_op jit(solution)/shard_map/reduce_scatter | solution.py:106
  484.8 62.2 %copy-start.3 = (bf16[1,16,4096]{2,1,0:T(8,128)(2,1)S(1)}, bf16[1,16,4096]{2,1,0:T(8,128)(2,1)}, u32[]{:S(2)}) copy-start(bf16[1,16,4096]{2,1,0:T(8,128)(2,1)} %reduce-scatter.6.cloned.1.call-done) | copy-start | bytes 393220
  484.8 65.6 %copy-start.2 = (bf16[1,256,4096]{2,1,0:T(8,128)(2,1)S(1)}, bf16[1,256,4096]{2,1,0:T(8,128)(2,1)}, u32[]{:S(2)}) copy-start(bf16[1,256,4096]{2,1,0:T(8,128)(2,1)} %all-gather.8.cloned.1.call-done) | copy-start | bytes 6291460
  484.8 140.4 %all-gather.14.cloned.1.call-start = ((), (), s32[]{:S(2)}) async-start(), calls=%async_computation.14 | async-start | bytes 2228224 | tf_op jit(solution)/shard_map/all_gather | solution.py:109
  550.3 166.8 %all-reduce.3.cloned.1.call-start = ((), (), s32[]{:S(2)}) async-start(), calls=%async_computation.15 | async-start | bytes 262144 | tf_op jit(solution)/shard_map/psum | solution.py:113
  550.4 7.0 copy-start.5
  550.4 7.0 copy-start.6
  557.4 6.0 copy-start.15
  557.4 6.0 copy-start.17
  566.3 56.8 %copy-start.4 = (bf16[1,256,4096]{2,1,0:T(8,128)(2,1)S(1)}, bf16[1,256,4096]{2,1,0:T(8,128)(2,1)}, u32[]{:S(2)}) copy-start(bf16[1,256,4096]{2,1,0:T(8,128)(2,1)} %all-gather.12.cloned.1.call-done) | copy-start | bytes 6291460
  625.2 102.5 %copy-start.1 = (bf16[256,4096]{1,0:T(8,128)(2,1)S(1)}, bf16[256,4096]{1,0:T(8,128)(2,1)}, u32[]{:S(2)}) copy-start(bf16[256,4096]{1,0:T(8,128)(2,1)} %param.26) | copy-start | bytes 6291460
  (16 other events, 32.3 us)
Sparse Core Ops, SparseCore 0:
  20.0 64.5 reduce-scatter.5
  89.1 40.6 all-gather.5
  139.7 60.2 reduce-scatter.7
  202.6 40.7 all-gather.7
  245.4 40.2 all-gather.9
  301.4 60.2 reduce-scatter.11
  366.0 60.7 reduce-scatter.9
  430.0 40.6 all-gather.11
  484.9 60.2 reduce-scatter.13
  550.4 40.7 all-gather.13
  625.3 91.7 all-reduce.2
where the time goes:
time: 735 us; the launch traced here: 734 us
  waiting for transfers between devices  544 us (74%)
  local copies, waits for them, and re-layouts  77.4 us (11%)
  matrix products  75.3 us (10%)
  other arithmetic  22.1 us (3%)
  between operations  14.3 us (2%)
    psum x1, waiting for transfers between devices, device_step(): lax.psum((d_emb_gain, d_emb_bias, d_ln1_gain, d_ln1_bias, jnp.sum(dr1_f32...  85.4 us
    unnamed x84, local copies, waits for them, and re-layouts  69.4 us
    reduce_scatter x1, waiting for transfers between devices, device_step(): emb_sum = lax.psum_scatter(emb_part, 'tp', scatter_dimension=1, tiled=True)  64.6 us
    reduce_scatter x1, waiting for transfers between devices, device_step(): mlp_sum = lax.psum_scatter(mlp_part, 'tp', scatter_dimension=1, tiled=True)  63.4 us
    reduce_scatter x1, waiting for transfers between devices, device_step(): dh1_sum = lax.psum_scatter(dh1_part, 'tp', scatter_dimension=1, tiled=True)  60.4 us
    reduce_scatter x1, waiting for transfers between devices, device_step(): lax.psum_scatter(dense_part, 'tp', scatter_dimension=1, tiled=True)  60.4 us
    reduce_scatter x1, waiting for transfers between devices, device_step(): dh2_sum = lax.psum_scatter(dh2_part, 'tp', scatter_dimension=1, tiled=True)  52.8 us
    all_gather x1, waiting for transfers between devices, device_step(): lax.all_gather(n1_norm.astype(jnp.bfloat16), 'tp', axis=1, tiled=True)  40.6 us
  transfers between devices with their start and end apart: 11, of which 10 were waited for; matrix products, arithmetic and copies ran while one was open for 13% of the time, Pallas kernels for 0%

commit v1 on v0

v1 whole, which is shorter than its diff:
```python
import functools
import jax
import jax.numpy as jnp
from jax import lax
from jax.experimental import pallas as pl
from jax.experimental.pallas import tpu as pltpu
from jax.sharding import PartitionSpec as P

EPS = 1e-5
MESH = pl.DeviceIdType.MESH
F32 = jnp.float32
BF16 = jnp.bfloat16
NCH = 4
NB = 16
BLK = 16
SEQ = 256
LANE = 128
QKV = 6 * LANE
ALL = slice(None)
GELU_A = 0.7978845608028654
GELU_B = 0.044715


def alibi_slopes(head_count):
    closest = 2 ** (head_count.bit_length() - 1)
    slope_base = 2.0 ** (-8.0 / closest)
    extra_base = 2.0 ** (-4.0 / closest)
    slopes = [slope_base ** exponent for exponent in range(1, closest + 1)]
    slopes = slopes + [extra_base ** exponent for exponent in range(1, 2 * (head_count - closest), 2)]
    return jnp.array(slopes, dtype=jnp.float32)


def norm_forward(values, gain_vec, bias_vec):
    centered = values - jnp.mean(values, axis=-1, keepdims=True)
    inv_std = lax.rsqrt(jnp.mean(centered * centered, axis=-1, keepdims=True) + EPS)
    x_hat = centered * inv_std
    return x_hat * gain_vec + bias_vec, x_hat, inv_std


def norm_backward(d_norm, x_hat, inv_std, gain_vec):
    d_hat = d_norm * gain_vec
    d_values = inv_std * (d_hat - jnp.mean(d_hat, axis=-1, keepdims=True)
                          - x_hat * jnp.mean(d_hat * x_hat, axis=-1, keepdims=True))
    return d_values, jnp.sum(d_norm * x_hat, axis=0, keepdims=True), jnp.sum(d_norm, axis=0, keepdims=True)


def dot_nn(a, b):
    return lax.dot_general(a, b, (((1,), (0,)), ((), ())), preferred_element_type=F32)


def dot_nt(a, b):
    return lax.dot_general(a, b, (((1,), (1,)), ((), ())), preferred_element_type=F32)


def dot_tn(a, b):
    return lax.dot_general(a, b, (((0,), (0,)), ((), ())), preferred_element_type=F32)


class Place:
    def __init__(self):
        t = lax.axis_index('tp')
        self.t = t
        self.c = lax.rem(t, 2)
        self.y = lax.rem(lax.div(t, 2), 2)
        self.z = lax.div(t, 4)
        self.sib = t + 1 - 2 * self.c
        self.yp = t + 2 - 4 * self.y
        self.zs = [self.z, self.z + 1 - 2 * lax.rem(self.z, 2), lax.rem(self.z + 2, 4), 3 - self.z]
        self.tz = [zk * 4 + self.y * 2 + self.c for zk in self.zs]
        self.own = self.c * 8 + self.y * 4
        self.oth = self.c * 8 + (1 - self.y) * 4
        self.me = self.own + self.z


class Gather:
    def __init__(self, pc, buf, send, recv, nch):
        self.pc, self.buf, self.send, self.recv, self.nch = pc, buf, send, recv, nch
        self.cw = buf.shape[2] // nch

    def rc(self, first, count, ch, slot, dev):
        ref = self.buf.at[pl.ds(first, count), :, pl.ds(pl.multiple_of(ch * self.cw, self.cw), self.cw)]
        return pltpu.make_async_remote_copy(
            src_ref=ref, dst_ref=ref, send_sem=self.send.at[ch, slot], recv_sem=self.recv.at[ch, slot],
            device_id={'tp': dev}, device_id_type=MESH)

    def start(self):
        pc = self.pc

        def body(ch, _):
            self.rc(pc.me, 1, ch, 3, pc.yp).start()
            for k in (1, 2, 3):
                self.rc(pc.me, 1, ch, k - 1, pc.tz[k]).start()
            return 0
        lax.fori_loop(0, self.nch, body, 0)

    def a(self, ch):
        pc = self.pc
        for k in (1, 2, 3):
            self.rc(pc.own + pc.zs[k], 1, ch, k - 1, pc.tz[k]).wait_recv()
            self.rc(pc.own + pc.zs[k], 1, ch, 3 + k, pc.yp).start()
        self.rc(pc.own, 4, ch, 7, pc.sib).start()

    def b(self, ch):
        pc = self.pc
        for k in (0, 1, 2, 3):
            self.rc(pc.oth + pc.zs[k], 1, ch, 3 + k, pc.yp).wait_recv()
        self.rc(pc.oth, 4, ch, 8, pc.sib).start()

    def c(self, ch):
        pc = self.pc
        self.rc(pc.own, 4, ch, 7, pc.sib).wait_recv()
        self.rc(pc.oth, 4, ch, 8, pc.sib).wait_recv()

    def finish(self):
        pc = self.pc

        def body(ch, _):
            for slot in range(7):
                self.rc(pc.me, 1, ch, slot, pc.yp).wait_send()
            for slot in (7, 8):
                self.rc(pc.own, 4, ch, slot, pc.sib).wait_send()
            return 0
        lax.fori_loop(0, self.nch, body, 0)

    def run(self, consume, hook=None):
        def body(s, _):
            @pl.when(s < self.nch)
            def _():
                self.a(s)

            @pl.when((s >= 1) & (s <= self.nch))
            def _():
                self.b(s - 1)

            if hook is not None:
                hook(s)

            @pl.when(s >= 2)
            def _():
                self.c(s - 2)
                if consume is not None:
                    consume(s - 2)
            return 0
        lax.fori_loop(0, self.nch + 2, body, 0)
        self.finish()


class Scatter:
    def __init__(self, pc, part, bufs, send, recv, out):
        self.pc, self.part, self.send, self.recv, self.out = pc, part, send, recv, out
        self.ra, self.sb, self.rb, self.sc, self.rcv = bufs
        self.cw = part.shape[2] // NCH

    def cols(self, ch):
        return pl.ds(pl.multiple_of(ch * self.cw, self.cw), self.cw)

    def copy(self, src, dst, ch, slot, dev):
        return pltpu.make_async_remote_copy(
            src_ref=src, dst_ref=dst, send_sem=self.send.at[ch, slot], recv_sem=self.recv.at[ch, slot],
            device_id={'tp': dev}, device_id_type=MESH)

    def to_sib(self, ch):
        pc = self.pc
        return self.copy(self.part.at[pl.ds((1 - pc.c) * 8, 8), :, self.cols(ch)],
                         self.ra.at[:, :, self.cols(ch)], ch, 0, pc.sib)

    def to_y(self, ch):
        return self.copy(self.sb.at[:, :, self.cols(ch)], self.rb.at[:, :, self.cols(ch)], ch, 1, self.pc.yp)

    def to_z(self, ch, k):
        return self.copy(self.sc.at[k - 1, :, self.cols(ch)], self.rcv.at[k - 1, :, self.cols(ch)],
                         ch, 1 + k, self.pc.tz[k])

    def s0(self, ch):
        self.to_sib(ch).start()

    def s1(self, ch):
        pc, cols = self.pc, self.cols(ch)
        self.to_sib(ch).wait_recv()
        for k in range(4):
            self.sb[k, :, cols] = (self.part[pc.oth + k, :, cols].astype(F32)
                                   + self.ra[(1 - pc.y) * 4 + k, :, cols].astype(F32)).astype(BF16)
        self.to_y(ch).start()

    def pair(self, zk, cols):
        pc = self.pc
        return (self.part[pc.own + zk, :, cols].astype(F32) + self.ra[pc.y * 4 + zk, :, cols].astype(F32)
                + self.rb[zk, :, cols].astype(F32))

    def s2(self, ch):
        pc, cols = self.pc, self.cols(ch)
        self.to_y(ch).wait_recv()
        for k in (2, 3, 1):
            self.sc[k - 1, :, cols] = self.pair(pc.zs[k], cols).astype(BF16)
            self.to_z(ch, k).start()

    def s3(self, ch):
        pc, cols = self.pc, self.cols(ch)
        acc = self.pair(pc.z, cols)
        for k in (1, 2, 3):
            self.to_z(ch, k).wait_recv()
            acc = acc + self.rcv[k - 1, :, cols].astype(F32)
        self.out[:, cols] = acc

    def finish(self):
        def body(ch, _):
            self.to_sib(ch).wait_send()
            self.to_y(ch).wait_send()
            for k in (1, 2, 3):
                self.to_z(ch, k).wait_send()
            return 0
        lax.fori_loop(0, NCH, body, 0)

    def run(self, compute, hook=None):
        def body(s, _):
            @pl.when(s < NCH)
            def _():
                compute(s)
                self.s0(s)

            @pl.when((s >= 1) & (s <= NCH))
            def _():
                self.s1(s - 1)

            if hook is not None:
                hook(s)

            @pl.when((s >= 2) & (s <= NCH + 1))
            def _():
                self.s2(s - 2)

            @pl.when(s >= 3)
            def _():
                self.s3(s - 3)
            return 0
        lax.fori_loop(0, NCH + 3, body, 0)
        self.finish()


def chain_kernel(ids, slopes, eg, eb, g1, b1, g2, b2, bd, bf2, bqkv, bf1, dout,
                 table_h, wqkv_h, wd_h, w1_h, w2_h,
                 h1_o, h2_o, dy_o, dr_o, dx_o, ctx_o, gelu_o, dpre_o, dqkv_o, y_o, small_o, dbf1_o, dbqkv_o,
                 table, wraw, wq, wd, w1, w2, h1, h2, dy, dr, dx, st2, st4, part, party,
                 ra, sb, rb, sc, rcv, yra, ysb, yrb, ysc, yrcv,
                 onehot, wstage, qkv_acc, qkv, prob, ctx, pre, dgelu, gelu_bf, dpre, dqkv,
                 rsum, e_val, e_hat, n1_hat, n2_hat, r_one, dr_own, invs,
                 lsem, osem, ags, agr, agds, agdr, rss, rsr, rsys, rsyr, sts, strc):
    pc = Place()
    dim = table.shape[1]
    vocab_rows = table.shape[0]
    cw = dim // NCH

    loads = [pltpu.make_async_copy(table_h, table, lsem.at[0]),
             pltpu.make_async_copy(wd_h, wd, lsem.at[1]),
             pltpu.make_async_copy(w1_h, w1, lsem.at[2]),
             pltpu.make_async_copy(w2_h, w2, lsem.at[3])]
    raw_rows = wraw.shape[1]

    def raw_load(ch, slot):
        return pltpu.make_async_copy(wqkv_h.at[pl.ds(pl.multiple_of(ch * raw_rows, raw_rows), raw_rows), :],
                                     wraw.at[slot], lsem.at[4 + slot])

    loads[0].start()
    raw_load(0, 0).start()
    raw_load(1, 1).start()
    for cp in loads[1:]:
        cp.start()

    barrier = pltpu.get_barrier_semaphore()
    partners = [pc.sib, pc.yp] + pc.tz[1:]
    for dev in partners:
        pl.semaphore_signal(barrier, inc=1, device_id={'tp': dev}, device_id_type=MESH)

    local_ids = ids[ALL] - pc.t * vocab_rows
    onehot[ALL] = (local_ids == lax.broadcasted_iota(jnp.int32, (SEQ, vocab_rows), 1)).astype(F32).astype(BF16)
    pl.semaphore_wait(barrier, len(partners))
    loads[0].wait()

    def cols(ch):
        return pl.ds(pl.multiple_of(ch * cw, cw), cw)

    def blocks(value):
        return value.reshape(NB, BLK, value.shape[1])

    def rows(value):
        return value.reshape(SEQ, value.shape[2])

    main = (ra, sb, rb, sc, rcv)
    side = (yra, ysb, yrb, ysc, yrcv)
    scatter = Scatter(pc, part, main, rss, rsr, rsum)
    scatter_y = Scatter(pc, party, side, rsys, rsyr, rsum)

    def embed(ch):
        part[:, :, cols(ch)] = blocks(dot_nn(onehot[ALL], table[:, cols(ch)]).astype(BF16))

    def unpack_wqkv(s):
        @pl.when(s < NCH)
        def _():
            slot = lax.rem(s, 2)
            raw_load(s, slot).wait()

            def body(i, _):
                wstage[ALL] = wraw[slot, pl.ds(pl.multiple_of(i * QKV, QKV), QKV), :].astype(F32)
                out_row = pl.multiple_of(s * cw + i * LANE, LANE)
                for j in range(6):
                    wq[pl.ds(out_row, LANE), j * LANE:(j + 1) * LANE] = wstage[pl.ds(j, LANE, stride=6), :].astype(BF16)
                return 0
            lax.fori_loop(0, raw_rows // QKV, body, 0)

            @pl.when(s + 2 < NCH)
            def _():
                raw_load(s + 2, slot).start()

    scatter.run(embed, unpack_wqkv)
    e_norm, hat, inv = norm_forward(rsum[ALL], eg[ALL], eb[ALL])
    e_hat[ALL] = hat
    invs[0] = jnp.broadcast_to(inv, (BLK, LANE))
    embedded = e_norm.astype(BF16).astype(F32)
    e_val[ALL] = embedded
    n1_norm, hat, inv = norm_forward(embedded, g1[ALL], b1[ALL])
    n1_hat[ALL] = hat
    invs[1] = jnp.broadcast_to(inv, (BLK, LANE))
    h1[pc.me] = n1_norm.astype(BF16)

    gather = Gather(pc, h1, ags, agr, NCH)
    gather.start()
    dy[pc.me] = dout[ALL]
    qkv_acc[ALL] = jnp.zeros_like(qkv_acc)

    def use_h1(ch):
        qkv_acc[ALL] += dot_nn(rows(h1[:, :, cols(ch)]), wq[cols(ch), :])

    gather.run(use_h1)
    gather_dy = Gather(pc, dy, agds, agdr, NCH)
    gather_dy.start()
    out_h1 = pltpu.make_async_copy(h1, h1_o, osem.at[0])
    out_h1.start()

    def position(axis):
        r = lax.broadcasted_iota(jnp.int32, (SEQ, SEQ), axis)
        core, yy = lax.shift_right_logical(r, 7), lax.shift_right_logical(r, 6) & 1
        zz, w = lax.shift_right_logical(r, 4) & 3, r & 15
        return zz * 64 + yy * 32 + core * 16 + w

    q_pos, k_pos = position(0), position(1)
    rel = (k_pos - q_pos).astype(F32)
    causal = k_pos <= q_pos
    scale = LANE ** -0.5

    for j in range(6):
        qkv[:, j * LANE:(j + 1) * LANE] = (qkv_acc[:, j * LANE:(j + 1) * LANE] + bqkv[j // 2, j % 2:j % 2 + 1, :]).astype(BF16)

    def head_cols(kind, h):
        return slice((kind * 2 + h) * LANE, (kind * 2 + h + 1) * LANE)

    def attend(h):
        scores = dot_nt(qkv[:, head_cols(0, h)], qkv[:, head_cols(1, h)]) * scale
        scores = jnp.where(causal, scores + slopes[pc.t * 2 + h] * rel, -1e30)
        ex = jnp.exp(scores - jnp.max(scores, axis=-1, keepdims=True))
        p = ex / jnp.sum(ex, axis=-1, keepdims=True)
        prob[h] = p
        ctx[:, h * LANE:(h + 1) * LANE] = dot_nn(p.astype(BF16), qkv[:, head_cols(2, h)]).astype(BF16)

    attend(0)
    lax.fori_loop(0, NCH, lambda ch, u: (gather_dy.a(ch), u)[1], 0)
    attend(1)
    loads[1].wait()

    def dense(ch):
        part[:, :, cols(ch)] = blocks(dot_nn(ctx[ALL], wd[:, cols(ch)]).astype(BF16))

    dgelu[ALL] = jnp.zeros_like(dgelu)
    loads[3].wait()

    def use_dy(s):
        @pl.when(s < NCH)
        def _():
            gather_dy.b(s)

        @pl.when((s >= 1) & (s <= NCH))
        def _():
            gather_dy.c(s - 1)
            dgelu[ALL] += dot_nt(rows(dy[:, :, cols(s - 1)]), w2[:, cols(s - 1)])

    scatter.run(dense, use_dy)
    gather_dy.finish()
    out_dy = pltpu.make_async_copy(dy, dy_o, osem.at[1])
    out_dy.start()
    out_ctx = pltpu.make_async_copy(ctx, ctx_o, osem.at[2])
    out_ctx.start()

    r_val = (e_val[ALL] + rsum[ALL] + bd[ALL]).astype(BF16).astype(F32)
    r_one[ALL] = r_val
    n2_norm, hat, inv = norm_forward(r_val, g2[ALL], b2[ALL])
    n2_hat[ALL] = hat
    invs[2] = jnp.broadcast_to(inv, (BLK, LANE))
    h2[pc.me] = n2_norm.astype(BF16)
    gather = Gather(pc, h2, ags, agr, NCH)
    gather.start()
    pre[ALL] = jnp.zeros_like(pre)
    loads[2].wait()

    def use_h2(ch):
        pre[ALL] += dot_nn(rows(h2[:, :, cols(ch)]), w1[cols(ch), :])

    gather.run(use_h2)
    out_h2 = pltpu.make_async_copy(h2, h2_o, osem.at[3])
    out_h2.start()

    def act(i, total):
        rs = pl.ds(pl.multiple_of(i * 32, 32), 32)
        x = pre[rs, :] + bf1[ALL]
        th = jnp.tanh(GELU_A * (x + GELU_B * (x * x * x)))
        cdf = 0.5 * (1.0 + th)
        gelu_bf[rs, :] = (x * cdf).astype(BF16)
        slope = cdf + x * (0.5 * (1.0 - th * th)) * (GELU_A * (1.0 + 3.0 * GELU_B * (x * x)))
        d = dgelu[rs, :] * slope
        dpre[rs, :] = d.astype(BF16)
        return total + jnp.sum(d, axis=0, keepdims=True)

    dbf1_o[ALL] = lax.fori_loop(0, SEQ // 32, act, jnp.zeros((1, pre.shape[1]), F32))
    out_gelu = pltpu.make_async_copy(gelu_bf, gelu_o, osem.at[4])
    out_gelu.start()
    out_dpre = pltpu.make_async_copy(dpre, dpre_o, osem.at[5])
    out_dpre.start()

    def dh2(ch):
        part[:, :, cols(ch)] = blocks(dot_nt(dpre[ALL], w1[cols(ch), :]).astype(BF16))

    def mlp(s):
        @pl.when(s < NCH)
        def _():
            party[:, :, cols(s)] = blocks(dot_nn(gelu_bf[ALL], w2[:, cols(s)]).astype(BF16))

    scatter.run(dh2, mlp)
    dn, sg, sbv = norm_backward(rsum[ALL], n2_hat[ALL], invs[2, :, 0:1], g2[ALL])
    dr_val = dout[ALL].astype(F32) + dn
    dr_own[ALL] = dr_val
    dr[pc.me] = dr_val.astype(BF16)
    st2[pc.me] = jnp.concatenate([sg, sbv], axis=0).astype(BF16)
    gather = Gather(pc, dr, ags, agr, NCH)
    gather.start()
    gather_st = Gather(pc, st2, sts, strc, 1)
    gather_st.start()
    d_ctx = qkv_acc.at[:, 0:256]
    d_ctx[ALL] = jnp.zeros((SEQ, 256), F32)

    def use_dr(ch):
        d_ctx[ALL] += dot_nt(rows(dr[:, :, cols(ch)]), wd[:, cols(ch)])

    def y_start(s):
        @pl.when(s < NCH)
        def _():
            scatter_y.s0(s)

    gather.run(use_dr, y_start)
    out_dr = pltpu.make_async_copy(dr, dr_o, osem.at[6])
    out_dr.start()
    gather_st.a(0)
    lax.fori_loop(0, NCH, lambda ch, u: (scatter_y.s1(ch), u)[1], 0)
    gather_st.b(0)

    def attend_back(h):
        dc = d_ctx[:, h * LANE:(h + 1) * LANE].astype(BF16)
        p = prob[h]
        d_value = dot_tn(p.astype(BF16), dc)
        d_prob = dot_nt(dc, qkv[:, head_cols(2, h)])
        ds = p * (d_prob - jnp.sum(d_prob * p, axis=-1, keepdims=True))
        ds_bf = (ds * scale).astype(BF16)
        d_query = dot_nn(ds_bf, qkv[:, head_cols(1, h)])
        d_key = dot_tn(ds_bf, qkv[:, head_cols(0, h)])
        for kind, val in ((0, d_query), (1, d_key), (2, d_value)):
            dqkv[:, head_cols(kind, h)] = val.astype(BF16)
            dbqkv_o[kind, h:h + 1, :] = jnp.sum(val, axis=0, keepdims=True)

    attend_back(0)
    attend_back(1)
    out_dqkv = pltpu.make_async_copy(dqkv, dqkv_o, osem.at[7])
    out_dqkv.start()
    lax.fori_loop(0, NCH, lambda ch, u: (scatter_y.s2(ch), u)[1], 0)

    gather_st.c(0)
    gather_st.finish()

    def dh1(ch):
        part[:, :, cols(ch)] = blocks(dot_nt(dqkv[ALL], wq[cols(ch), :]).astype(BF16))

    scatter.run(dh1)
    dn, sg1, sb1 = norm_backward(rsum[ALL], n1_hat[ALL], invs[1, :, 0:1], g1[ALL])
    dxv, sg0, sb0 = norm_backward(dr_own[ALL] + dn, e_hat[ALL], invs[0, :, 0:1], eg[ALL])
    dx[pc.me] = dxv.astype(BF16)
    st4[pc.me] = jnp.concatenate([sg0, sb0, sg1, sb1], axis=0).astype(BF16)
    gather = Gather(pc, dx, ags, agr, NCH)
    gather.start()
    gather_st = Gather(pc, st4, sts, strc, 1)
    gather_st.start()

    lax.fori_loop(0, NCH, lambda ch, u: (scatter_y.s3(ch), u)[1], 0)
    scatter_y.finish()
    y_o[ALL] = (r_one[ALL] + rsum[ALL] + bf2[ALL]).astype(BF16)
    small_o[4:6, :] = jnp.sum(st2[ALL].astype(F32), axis=0)

    def col_sums(s):
        @pl.when(s < NCH)
        def _():
            small_o[6:7, cols(s)] = jnp.sum(rows(dr[:, :, cols(s)]).astype(F32), axis=0, keepdims=True)
            small_o[7:8, cols(s)] = jnp.sum(rows(dy[:, :, cols(s)]).astype(F32), axis=0, keepdims=True)

    gather.run(None, col_sums)
    gather_st.a(0)
    gather_st.b(0)
    gather_st.c(0)
    gather_st.finish()
    small_o[0:4, :] = jnp.sum(st4[ALL].astype(F32), axis=0)
    out_dx = pltpu.make_async_copy(dx, dx_o, osem.at[8])
    out_dx.start()
    for cp in (out_h1, out_dy, out_ctx, out_h2, out_gelu, out_dpre, out_dr, out_dqkv, out_dx):
        cp.wait()


def chain(ids, slopes, vecs, bqkv, bf1, dout, table, wqkv, wd, w1, w2):
    vocab_rows, dim = table.shape
    ff = w1.shape[1]
    act = jax.ShapeDtypeStruct((NB, BLK, dim), BF16)
    out_shape = [act] * 5 + [
        jax.ShapeDtypeStruct((SEQ, 256), BF16), jax.ShapeDtypeStruct((SEQ, ff), BF16),
        jax.ShapeDtypeStruct((SEQ, ff), BF16), jax.ShapeDtypeStruct((SEQ, QKV), BF16),
        jax.ShapeDtypeStruct((BLK, dim), BF16), jax.ShapeDtypeStruct((8, dim), F32),
        jax.ShapeDtypeStruct((1, ff), F32), jax.ShapeDtypeStruct((3, 2, LANE), F32)]
    vmem, hbm = pl.BlockSpec(memory_space=pltpu.VMEM), pl.BlockSpec(memory_space=pl.ANY)
    full = pltpu.VMEM((NB, BLK, dim), BF16)
    rs_bufs = [pltpu.VMEM((8, BLK, dim), BF16), pltpu.VMEM((4, BLK, dim), BF16), pltpu.VMEM((4, BLK, dim), BF16),
               pltpu.VMEM((3, BLK, dim), BF16), pltpu.VMEM((3, BLK, dim), BF16)]
    row = pltpu.VMEM((BLK, dim), F32)
    dma = pltpu.SemaphoreType.DMA
    scratch = [pltpu.VMEM((vocab_rows, dim), BF16), pltpu.VMEM((2, dim * 6 // NCH, LANE), BF16),
               pltpu.VMEM((dim, QKV), BF16), pltpu.VMEM(wd.shape, BF16), pltpu.VMEM(w1.shape, BF16),
               pltpu.VMEM(w2.shape, BF16), full, full, full, full, full,
               pltpu.VMEM((NB, 2, dim), BF16), pltpu.VMEM((NB, 4, dim), BF16), full, full]
    scratch += rs_bufs + rs_bufs
    scratch += [pltpu.VMEM((SEQ, vocab_rows), BF16), pltpu.VMEM((QKV, LANE), F32), pltpu.VMEM((SEQ, QKV), F32),
                pltpu.VMEM((SEQ, QKV), BF16), pltpu.VMEM((2, SEQ, SEQ), F32), pltpu.VMEM((SEQ, 256), BF16),
                pltpu.VMEM((SEQ, ff), F32), pltpu.VMEM((SEQ, ff), F32), pltpu.VMEM((SEQ, ff), BF16),
                pltpu.VMEM((SEQ, ff), BF16), pltpu.VMEM((SEQ, QKV), BF16)]
    scratch += [row] * 7 + [pltpu.VMEM((3, BLK, LANE), F32)]
    scratch += [dma((6,)), dma((9,)), dma((NCH, 9)), dma((NCH, 9)), dma((NCH, 9)), dma((NCH, 9)),
                dma((NCH, 5)), dma((NCH, 5)), dma((NCH, 5)), dma((NCH, 5)), dma((1, 9)), dma((1, 9))]
    return pl.pallas_call(
        chain_kernel, out_shape=out_shape,
        in_specs=[vmem, pl.BlockSpec(memory_space=pltpu.SMEM)] + [vmem] * 11 + [hbm] * 5,
        out_specs=[hbm] * 9 + [vmem] * 4,
        scratch_shapes=scratch, name='chain',
        compiler_params=pltpu.CompilerParams(collective_id=1, has_side_effects=True,
                                             vmem_limit_bytes=67043328),
    )(ids, slopes, *vecs, bqkv, bf1, dout, table, wqkv, wd, w1, w2)


def qkv_grad_kernel(h1, dqkv, out, stage):
    n = h1.shape[1]
    for j in range(6):
        stage[pl.ds(j, n, stride=6), :] = dot_tn(h1[ALL], dqkv[:, j * LANE:(j + 1) * LANE])
    out[ALL] = stage[ALL].astype(BF16)


def qkv_grad(h1, dqkv):
    dim = h1.shape[1]
    step = 512
    return pl.pallas_call(
        qkv_grad_kernel, out_shape=jax.ShapeDtypeStruct((dim * 6, LANE), BF16), grid=(dim // step,),
        in_specs=[pl.BlockSpec((SEQ, step), lambda i: (0, i)), pl.BlockSpec((SEQ, QKV), lambda i: (0, 0))],
        out_specs=pl.BlockSpec((step * 6, LANE), lambda i: (i, 0)),
        scratch_shapes=[pltpu.VMEM((step * 6, LANE), F32)], name='qkv_grad')(h1, dqkv)


def device_step(token_ids, embed_table, emb_gain, emb_bias, ln1_gain, ln1_bias,
                w_qkv, b_qkv, w_dense, b_dense, ln2_gain, ln2_bias,
                w_fc1, b_fc1, w_fc2, b_fc2, d_out, slopes_all):
    dim = embed_table.shape[1]
    vocab_rows = embed_table.shape[0]
    ids = token_ids.reshape(4, 2, 2, BLK).transpose(2, 1, 0, 3).reshape(SEQ, 1)
    vecs = [v.reshape(1, dim) for v in (emb_gain, emb_bias, ln1_gain, ln1_bias, ln2_gain, ln2_bias, b_dense, b_fc2)]
    wqkv = w_qkv.transpose(0, 2, 1, 3).reshape(dim * 6, LANE)
    (h1, h2, dy, dr, dx, ctx, gelu, dpre, dqkv, y, small, dbf1, dbqkv) = chain(
        ids, slopes_all, vecs, b_qkv.transpose(1, 0, 2), b_fc1.reshape(1, -1), d_out.reshape(BLK, dim),
        embed_table, wqkv, w_dense, w_fc1, w_fc2)
    h1, h2, dy, dr, dx = (v.reshape(SEQ, dim) for v in (h1, h2, dy, dr, dx))
    d_w_qkv = qkv_grad(h1, dqkv).reshape(dim, 3, 2, LANE).transpose(0, 2, 1, 3)
    d_w_fc2 = dot_tn(gelu, dy).astype(BF16)
    d_w_fc1 = dot_tn(h2, dpre).astype(BF16)
    d_w_dense = dot_tn(ctx, dr).astype(BF16)
    one_hot = (ids - lax.axis_index('tp') * vocab_rows == jnp.arange(vocab_rows)[None, :]).astype(BF16)
    d_table = dot_tn(one_hot, dx)
    return (y[None], d_table, small[0], small[1], small[2], small[3],
            d_w_qkv, dbqkv.transpose(1, 0, 2), d_w_dense, small[6], small[4], small[5],
            d_w_fc1, dbf1.reshape(-1), d_w_fc2, small[7])


def solution(mesh):
    in_specs = (P('dp', None), P('tp', None), P(None), P(None), P(None), P(None),
                P(None, 'tp', None, None), P('tp', None, None), P('tp', None), P(None),
                P(None), P(None), P(None, 'tp'), P('tp'), P('tp', None), P(None),
                P('dp', 'tp', None), P(None))
    out_specs = (P('dp', 'tp', None), P(('dp', 'tp'), None), P('dp'), P('dp'), P('dp'), P('dp'),
                 P('dp', 'tp', None, None), P(('dp', 'tp'), None, None), P(('dp', 'tp'), None), P('dp'),
                 P('dp'), P('dp'), P('dp', 'tp'), P(('dp', 'tp')), P(('dp', 'tp'), None), P('dp'))
    mapped = jax.shard_map(device_step, mesh=mesh, in_specs=in_specs, out_specs=out_specs, check_vma=False)

    def run(*arrays):
        slopes_all = alibi_slopes(arrays[6].shape[1])
        return mapped(*arrays, slopes_all)

    return run
```

time: 735 us -> 251 us (0.34)
  waiting for transfers between devices: 544 us -> 0 us
  Pallas kernels: 0 us -> 222 us
  local copies, waits for them, and re-layouts: 77.4 us -> 4.62 us
  matrix products: 75.3 us -> 22 us
  other arithmetic: 22.1 us -> 1.34 us
  between operations: 14.3 us -> 0.73 us
    reduce_scatter x5 -> x0, waiting for transfers between devices: 302 us -> none  [the longest x1 64.6 us: device_step(): emb_sum = lax.psum_scatter(emb_part, 'tp', scatter_dimension=1, tiled=True)]
    pallas_call x0 -> x2, Pallas kernels: none -> 222 us  [the longest x1 212 us: chain(): pl.pallas_call(chain_kernel, out_shape=out_shape, in_specs=[vmem, pl.Bloc...]
    all_gather x5 -> x0, waiting for transfers between devices: 157 us -> none  [the longest x1 40.6 us: device_step(): lax.all_gather(n1_norm.astype(jnp.bfloat16), 'tp', axis=1, tiled=True)]
    psum x1 -> x0, waiting for transfers between devices: 85.4 us -> none  [device_step(): lax.psum((d_emb_gain, d_emb_bias, d_ln1_gain, d_ln1_bias, jnp.sum(dr1_f32...]
    unnamed x84 -> x24, local copies, waits for them, and re-layouts: 69.4 us -> 2.97 us
    dot_general x19 -> x4, matrix products: 75.3 us -> 22 us  [dot_tn(): lax.dot_general(a, b, (((0,), (0,)), ((), ())), preferred_element_type=F32)]
    reduce_sum x11 -> x0, other arithmetic: 13.2 us -> none  [the longest x3 5.24 us: norm_backward(): jnp.sum(d_norm * x_hat, axis=(0, 1))]
    gather x1 -> x0, local copies, waits for them, and re-layouts: 7.93 us -> none  [device_step(): jnp.take(embed_table, jnp.clip(local_ids, 0, vocab_rows - 1), axis=0)]
  transfers between devices with their start and end apart: 11 -> 0, of which waited for: 10 -> 0; matrix products, arithmetic and copies ran while one was open for 13% -> 0% of each run, Pallas kernels for 0% -> 0%
where the time goes in v1:
time: 251 us; the launch traced here: 250 us
  Pallas kernels  222 us (88%)
  matrix products  22 us (9%)
  local copies, waits for them, and re-layouts  4.62 us (2%)
    pallas_call x1, Pallas kernels, chain(): pl.pallas_call(chain_kernel, out_shape=out_shape, in_specs=[vmem, pl.Bloc...  212 us
    dot_general x4, matrix products, dot_tn(): lax.dot_general(a, b, (((0,), (0,)), ((), ())), preferred_element_type=F32)  22 us
    pallas_call x1, Pallas kernels, qkv_grad(): pl.pallas_call(qkv_grad_kernel, out_shape=jax.ShapeDtypeStruct((dim * 6,...  9.09 us

profile of v1, /device:TPU:0, one launch (start us, length us, event | category | flops | bytes accessed | tf_op | source)
XLA Modules:
  0.0 250.3 jit_solution(12452134093678074304)
XLA Ops:
  0.6 0.5 broadcast.10
  1.2 1.3 reduce.3
  2.5 0.1 reshape.101
  2.6 0.0 copy-start.6
  2.6 0.6 copy-done.6
  3.2 0.8 reshape.121.ids
  4.0 212.5 %chain.1 = (bf16[16,16,4096]{2,1,0:T(8,128)(2,1)}, bf16[16,16,4096]{2,1,0:T(8,128)(2,1)}, bf16[16,16,4096]{2,1,0:T(8,128)(2,1)}, bf16[16,16,4096]{2,1,0:T(8,128)...) custom-call(s32[256,1]{1,0:T(8,128)} %reshape.121.ids, ...), custom_call_target="tpu_custom_call" | custom-call | tf_op jit(solution)/shard_map/chain/pallas_call | solution.py:548
  216.5 0.0 copy-start
  216.5 0.0 copy-start.2
  216.5 7.7 %convolution_convert_fusion = bf16[1024,4096]{1,0:T(8,128)(2,1)} fusion(bf16[256,1024]{1,0:T(8,128)(2,1)} %get-tuple-element.40, bf16[256,4096]{1,0:T(8,128)(2,1)} %bitcast.51), kind=kOutput, calls=%fused_computation | convolution fusion | flops 2151677952 | bytes 11010048 | tf_op jit(solution)/shard_map/dot_general | solution.py:56
  224.2 0.0 copy-done
  224.2 0.0 copy-done.2
  224.2 5.8 %convolution_convert_fusion.1 = bf16[4096,1024]{1,0:T(8,128)(2,1)} fusion(bf16[256,4096]{1,0:T(8,128)(2,1)S(1)} %bitcast.47, bf16[256,1024]{1,0:T(8,128)(2,1)S(1)} %copy-done.2), kind=kOutput, calls=%fused_computation.1 | convolution fusion | flops 2151677952 | bytes 11010048 | tf_op jit(solution)/shard_map/dot_general | solution.py:56
  229.9 0.0 copy-start.3
  230.0 9.1 %qkv_grad.1 = bf16[24576,128]{1,0:T(8,128)(2,1)} custom-call(bf16[256,4096]{1,0:T(8,128)(2,1)} %bitcast.50, bf16[256,768]{1,0:T(8,128)(2,1)} %get-tuple-element.33.dqkv), custom_call_target="tpu_custom_call" | custom-call | tf_op jit(solution)/shard_map/qkv_grad/pallas_call | solution.py:568
  239.0 0.0 copy-done.3
  239.0 0.0 copy-start.1
  239.1 3.8 %convolution_convert_fusion.2 = bf16[256,4096]{1,0:T(8,128)(2,1)} fusion(bf16[256,256]{1,0:T(8,128)(2,1)S(1)} %copy-done.3, bf16[256,4096]{1,0:T(8,128)(2,1)} %bitcast.49), kind=kOutput, calls=%fused_computation.2 | convolution fusion | flops 537919488 | bytes 4325376 | tf_op jit(solution)/shard_map/dot_general | solution.py:56
  242.9 0.0 copy-done.5
  242.9 0.7 fusion.2
  243.6 0.0 copy-done.7
  243.6 0.1 sub.16
  243.7 0.0 copy-done.1
  243.7 0.0 copy-start.9
  243.7 0.0 copy-start.8
  243.7 4.8 %fusion = f32[512,4096]{1,0:T(8,128)} fusion(bf16[256,4096]{1,0:T(8,128)(2,1)S(1)} %bitcast.48, s32[256]{0:T(256)S(1)} %sub.16), kind=kOutput, calls=%fused_computation.4 | convolution fusion | flops 1073872896 | bytes 10486784 | tf_op jit(solution)/shard_map/dot_general | solution.py:56
  248.5 0.0 copy-done.4
  248.5 0.7 copy.44
  249.1 0.0 copy-done.9
  249.1 0.6 copy.45
  249.7 0.0 copy-done.8
  249.7 0.6 copy.46
  (5 shorter events, 0.0 us)
Async XLA Ops:
  2.6 0.6 copy-start.6
  216.5 7.7 %copy-start = (bf16[16,16,4096]{2,1,0:T(8,128)(2,1)S(1)}, bf16[16,16,4096]{2,1,0:T(8,128)(2,1)}, u32[]{:S(2)}) copy-start(bf16[16,16,4096]{2,1,0:T(8,128)(2,1)} %get-tuple-element.37) | copy-start | bytes 6291460
  216.5 7.7 %copy-start.2 = (bf16[256,1024]{1,0:T(8,128)(2,1)S(1)}, bf16[256,1024]{1,0:T(8,128)(2,1)}, u32[]{:S(2)}) copy-start(bf16[256,1024]{1,0:T(8,128)(2,1)} %get-tuple-element.38) | copy-start | bytes 1572868
  229.9 9.1 %copy-start.3 = (bf16[256,256]{1,0:T(8,128)(2,1)S(1)}, bf16[256,256]{1,0:T(8,128)(2,1)}, u32[]{:S(2)}) copy-start(bf16[256,256]{1,0:T(8,128)(2,1)} %get-tuple-element.35) | copy-start | bytes 393220
  239.0 3.8 %copy-start.5 = (f32[8,4096]{1,0:T(8,128)S(1)}, f32[8,4096]{1,0:T(8,128)}, u32[]{:S(2)}) copy-start(f32[8,4096]{1,0:T(8,128)} %get-tuple-element.31) | copy-start | bytes 393220
  239.0 4.5 %copy-start.7 = (s32[4,2,2,16]{3,2,1,0:T(2,128)S(1)}, s32[4,2,2,16]{3,2,1,0:T(2,128)}, u32[]{:S(2)}) copy-start(s32[4,2,2,16]{3,2,1,0:T(2,128)} %copy-done.6) | copy-start | bytes 3076
  239.0 4.6 %copy-start.1 = (bf16[16,16,4096]{2,1,0:T(8,128)(2,1)S(1)}, bf16[16,16,4096]{2,1,0:T(8,128)(2,1)}, u32[]{:S(2)}) copy-start(bf16[16,16,4096]{2,1,0:T(8,128)(2,1)} %get-tuple-element.30) | copy-start | bytes 6291460
  243.7 4.8 %copy-start.4 = (bf16[16,4096]{1,0:T(8,128)(2,1)S(1)}, bf16[16,4096]{1,0:T(8,128)(2,1)}, u32[]{:S(2)}) copy-start(bf16[16,4096]{1,0:T(8,128)(2,1)} %get-tuple-element.29) | copy-start | bytes 393220
  243.7 5.5 %copy-start.9 = (f32[3,2,128]{2,1,0:T(2,128)S(1)}, f32[3,2,128]{2,1,0:T(2,128)}, u32[]{:S(2)}) copy-start(f32[3,2,128]{2,1,0:T(2,128)} %get-tuple-element.34) | copy-start | bytes 9220
  243.7 6.0 %copy-start.8 = (f32[1,1024]{1,0:T(1,128)S(1)}, f32[1,1024]{1,0:T(1,128)}, u32[]{:S(2)}) copy-start(f32[1,1024]{1,0:T(1,128)} %get-tuple-element.39) | copy-start | bytes 12292

commit v2 on v1

--- a/solution.py
+++ b/solution.py
@@ -10,7 +10,9 @@
 MESH = pl.DeviceIdType.MESH
 F32 = jnp.float32
 BF16 = jnp.bfloat16
-NCH = 4
+NA = 4
+NR = 4
+NW = 4
 NB = 16
 BLK = 16
 SEQ = 256
@@ -63,6 +65,8 @@
         self.c = lax.rem(t, 2)
         self.y = lax.rem(lax.div(t, 2), 2)
         self.z = lax.div(t, 4)
+        self.inner = (self.z == 1) | (self.z == 2)
+        self.end = (self.z == 0) | (self.z == 3)
         self.sib = t + 1 - 2 * self.c
         self.yp = t + 2 - 4 * self.y
         self.zs = [self.z, self.z + 1 - 2 * lax.rem(self.z, 2), lax.rem(self.z + 2, 4), 3 - self.z]
@@ -72,37 +76,81 @@
         self.me = self.own + self.z
 
 
+def remote(src, dst, send_sem, recv_sem, dev):
+    return pltpu.make_async_remote_copy(src_ref=src, dst_ref=dst, send_sem=send_sem, recv_sem=recv_sem,
+                                        device_id={'tp': dev}, device_id_type=MESH)
+
+
+def loop(n, fn):
+    def body(i, carry):
+        fn(i)
+        return carry
+    lax.fori_loop(0, n, body, 0)
+
+
 class Gather:
-    def __init__(self, pc, buf, send, recv, nch):
-        self.pc, self.buf, self.send, self.recv, self.nch = pc, buf, send, recv, nch
-        self.cw = buf.shape[2] // nch
-
-    def rc(self, first, count, ch, slot, dev):
+    def __init__(self, pc, buf, send, recv):
+        self.pc, self.buf, self.send, self.recv = pc, buf, send, recv
+        self.cw = buf.shape[2] // NA
+
+    def rc(self, first, count, ch, slot, dev, send_slot=None):
         ref = self.buf.at[pl.ds(first, count), :, pl.ds(pl.multiple_of(ch * self.cw, self.cw), self.cw)]
-        return pltpu.make_async_remote_copy(
-            src_ref=ref, dst_ref=ref, send_sem=self.send.at[ch, slot], recv_sem=self.recv.at[ch, slot],
-            device_id={'tp': dev}, device_id_type=MESH)
+        send_slot = slot if send_slot is None else send_slot
+        return remote(ref, ref, self.send.at[ch, send_slot], self.recv.at[ch, slot], dev)
+
+    def block(self, k, ch):
+        return self.rc(self.pc.own + self.pc.zs[k], 1, ch, k - 1, self.pc.tz[k])
+
+    def start_y(self):
+        loop(NA, lambda ch: self.rc(self.pc.me, 1, ch, 3, self.pc.yp).start())
+
+    def start_z(self):
+        pc = self.pc
+
+        def body(ch):
+            self.rc(pc.me, 1, ch, 0, pc.tz[1]).start()
+
+            @pl.when(pc.inner)
+            def _():
+                self.rc(pc.me, 1, ch, 2, pc.tz[3]).start()
+
+            @pl.when(pc.end)
+            def _():
+                self.rc(pc.me, 1, ch, 1, pc.tz[2]).start()
+        loop(NA, body)
 
     def start(self):
-        pc = self.pc
-
-        def body(ch, _):
-            self.rc(pc.me, 1, ch, 3, pc.yp).start()
-            for k in (1, 2, 3):
-                self.rc(pc.me, 1, ch, k - 1, pc.tz[k]).start()
-            return 0
-        lax.fori_loop(0, self.nch, body, 0)
+        self.start_y()
+        self.start_z()
+
+    def to_y(self, k, ch):
+        self.rc(self.pc.own + self.pc.zs[k], 1, ch, 3 + k, self.pc.yp).start()
+
+    def to_end(self, k, ch):
+        self.rc(self.pc.own + self.pc.zs[k], 1, ch, 4 - k, self.pc.tz[1], 7 + k).start()
 
     def a(self, ch):
         pc = self.pc
-        for k in (1, 2, 3):
-            self.rc(pc.own + pc.zs[k], 1, ch, k - 1, pc.tz[k]).wait_recv()
-            self.rc(pc.own + pc.zs[k], 1, ch, 3 + k, pc.yp).start()
+        self.block(1, ch).wait_recv()
+        self.to_y(1, ch)
+
+        @pl.when(pc.inner)
+        def _():
+            for k in (3, 2):
+                self.block(k, ch).wait_recv()
+                self.to_end(k, ch)
+                self.to_y(k, ch)
+
+        @pl.when(pc.end)
+        def _():
+            for k in (2, 3):
+                self.block(k, ch).wait_recv()
+                self.to_y(k, ch)
         self.rc(pc.own, 4, ch, 7, pc.sib).start()
 
     def b(self, ch):
         pc = self.pc
-        for k in (0, 1, 2, 3):
+        for k in range(4):
             self.rc(pc.oth + pc.zs[k], 1, ch, 3 + k, pc.yp).wait_recv()
         self.rc(pc.oth, 4, ch, 8, pc.sib).start()
 
@@ -114,21 +162,34 @@
     def finish(self):
         pc = self.pc
 
-        def body(ch, _):
-            for slot in range(7):
+        def body(ch):
+            for slot in (0, 3, 4, 5, 6):
                 self.rc(pc.me, 1, ch, slot, pc.yp).wait_send()
+
+            @pl.when(pc.inner)
+            def _():
+                for slot in (2, 9, 10):
+                    self.rc(pc.me, 1, ch, 0, pc.yp, slot).wait_send()
+
+            @pl.when(pc.end)
+            def _():
+                self.rc(pc.me, 1, ch, 1, pc.yp).wait_send()
             for slot in (7, 8):
                 self.rc(pc.own, 4, ch, slot, pc.sib).wait_send()
-            return 0
-        lax.fori_loop(0, self.nch, body, 0)
-
-    def run(self, consume, hook=None):
-        def body(s, _):
-            @pl.when(s < self.nch)
+        loop(NA, body)
+
+    def run(self, consume, after_a=None, hook=None):
+        def body(s):
+            @pl.when(s < NA)
             def _():
                 self.a(s)
 
-            @pl.when((s >= 1) & (s <= self.nch))
+            if after_a is not None:
+                @pl.when(s == NA)
+                def _():
+                    after_a()
+
+            @pl.when((s >= 1) & (s <= NA))
             def _():
                 self.b(s - 1)
 
@@ -140,8 +201,7 @@
                 self.c(s - 2)
                 if consume is not None:
                     consume(s - 2)
-            return 0
-        lax.fori_loop(0, self.nch + 2, body, 0)
+        loop(NA + 2, body)
         self.finish()
 
 
@@ -149,15 +209,13 @@
     def __init__(self, pc, part, bufs, send, recv, out):
         self.pc, self.part, self.send, self.recv, self.out = pc, part, send, recv, out
         self.ra, self.sb, self.rb, self.sc, self.rcv = bufs
-        self.cw = part.shape[2] // NCH
+        self.cw = part.shape[2] // NR
 
     def cols(self, ch):
         return pl.ds(pl.multiple_of(ch * self.cw, self.cw), self.cw)
 
     def copy(self, src, dst, ch, slot, dev):
-        return pltpu.make_async_remote_copy(
-            src_ref=src, dst_ref=dst, send_sem=self.send.at[ch, slot], recv_sem=self.recv.at[ch, slot],
-            device_id={'tp': dev}, device_id_type=MESH)
+        return remote(src, dst, self.send.at[ch, slot], self.recv.at[ch, slot], dev)
 
     def to_sib(self, ch):
         pc = self.pc
@@ -203,52 +261,108 @@
         self.out[:, cols] = acc
 
     def finish(self):
-        def body(ch, _):
+        def body(ch):
             self.to_sib(ch).wait_send()
             self.to_y(ch).wait_send()
             for k in (1, 2, 3):
                 self.to_z(ch, k).wait_send()
-            return 0
-        lax.fori_loop(0, NCH, body, 0)
-
-    def run(self, compute, hook=None):
-        def body(s, _):
-            @pl.when(s < NCH)
+        loop(NR, body)
+
+    def run(self, compute, hook=None, mid=None):
+        def front(s):
+            @pl.when(s < NR)
             def _():
                 compute(s)
                 self.s0(s)
 
-            @pl.when((s >= 1) & (s <= NCH))
+            @pl.when(s >= 1)
             def _():
                 self.s1(s - 1)
-
+        loop(NR + 1, front)
+
+        def back(s):
             if hook is not None:
                 hook(s)
-
-            @pl.when((s >= 2) & (s <= NCH + 1))
-            def _():
-                self.s2(s - 2)
-
-            @pl.when(s >= 3)
-            def _():
-                self.s3(s - 3)
-            return 0
-        lax.fori_loop(0, NCH + 3, body, 0)
+            self.s2(s)
+        loop(NR, back)
+        if mid is not None:
+            mid()
+        loop(NR, self.s3)
         self.finish()
+
+
+class SmallSum:
+    def __init__(self, pc, rows_f32, vals, ra, sb, rb, rz, total, send, recv):
+        self.pc, self.rows, self.vals, self.ra, self.sb, self.rb, self.rz = pc, rows_f32, vals, ra, sb, rb, rz
+        self.total, self.send, self.recv = total, send, recv
+        self.half = vals.shape[1] // 2
+
+    def cols(self, core):
+        return pl.ds(pl.multiple_of(core * self.half, self.half), self.half)
+
+    def copy(self, src, dst, slot, dev):
+        return remote(src, dst, self.send.at[slot], self.recv.at[slot], dev)
+
+    def to_sib(self):
+        return self.copy(self.vals.at[:, self.cols(1 - self.pc.c)], self.ra, 0, self.pc.sib)
+
+    def to_y(self):
+        return self.copy(self.sb, self.rb, 1, self.pc.yp)
+
+    def to_z(self, k):
+        return self.copy(self.rz.at[self.pc.z], self.rz.at[self.pc.z], 1 + k, self.pc.tz[k])
+
+    def back(self):
+        ref = self.total.at[:, self.cols(self.pc.c)]
+        return self.copy(ref, ref, 5, self.pc.sib)
+
+    def t0(self):
+        self.vals[ALL] = self.rows[ALL].astype(BF16)
+        self.to_sib().start()
+
+    def t1(self):
+        self.to_sib().wait_recv()
+        self.sb[ALL] = (self.vals[:, self.cols(self.pc.c)].astype(F32) + self.ra[ALL].astype(F32)).astype(BF16)
+        self.to_y().start()
+
+    def t2(self):
+        self.to_y().wait_recv()
+        self.rz[self.pc.z] = (self.sb[ALL].astype(F32) + self.rb[ALL].astype(F32)).astype(BF16)
+        for k in (1, 2, 3):
+            self.to_z(k).start()
+
+    def t3(self):
+        for k in (1, 2, 3):
+            self.to_z(k).wait_recv()
+        self.total[:, self.cols(self.pc.c)] = jnp.sum(self.rz[ALL].astype(F32), axis=0)
+        self.back().start()
+
+    def t4(self):
+        self.back().wait_recv()
+        self.back().wait_send()
+        self.to_sib().wait_send()
+        self.to_y().wait_send()
+        for k in (1, 2, 3):
+            self.to_z(k).wait_send()
+
+
+def block_of(t):
+    return (t % 2) * 8 + (t // 2 % 2) * 4 + t // 4
 
 
 def chain_kernel(ids, slopes, eg, eb, g1, b1, g2, b2, bd, bf2, bqkv, bf1, dout,
                  table_h, wqkv_h, wd_h, w1_h, w2_h,
                  h1_o, h2_o, dy_o, dr_o, dx_o, ctx_o, gelu_o, dpre_o, dqkv_o, y_o, small_o, dbf1_o, dbqkv_o,
-                 table, wraw, wq, wd, w1, w2, h1, h2, dy, dr, dx, st2, st4, part, party,
+                 table, wraw, wq, wd, w1, w2, h1, h2, dy, dr, dx, part, party,
                  ra, sb, rb, sc, rcv, yra, ysb, yrb, ysc, yrcv,
                  onehot, wstage, qkv_acc, qkv, prob, ctx, pre, dgelu, gelu_bf, dpre, dqkv,
                  rsum, e_val, e_hat, n1_hat, n2_hat, r_one, dr_own, invs,
+                 stat, sv, sra, ssb, srb, srz, stot,
                  lsem, osem, ags, agr, agds, agdr, rss, rsr, rsys, rsyr, sts, strc):
     pc = Place()
     dim = table.shape[1]
     vocab_rows = table.shape[0]
-    cw = dim // NCH
+    ra_w, rs_w, wq_w = dim // NA, dim // NR, dim // NW
 
     loads = [pltpu.make_async_copy(table_h, table, lsem.at[0]),
              pltpu.make_async_copy(wd_h, wd, lsem.at[1]),
@@ -272,12 +386,17 @@
         pl.semaphore_signal(barrier, inc=1, device_id={'tp': dev}, device_id_type=MESH)
 
     local_ids = ids[ALL] - pc.t * vocab_rows
-    onehot[ALL] = (local_ids == lax.broadcasted_iota(jnp.int32, (SEQ, vocab_rows), 1)).astype(F32).astype(BF16)
+    hit = (local_ids == lax.broadcasted_iota(jnp.int32, (vocab_rows, SEQ), 0)).astype(F32).T.astype(BF16)
+    for t in range(NB):
+        onehot[block_of(t) * BLK:(block_of(t) + 1) * BLK, :] = hit[t * BLK:(t + 1) * BLK, :]
     pl.semaphore_wait(barrier, len(partners))
     loads[0].wait()
 
-    def cols(ch):
-        return pl.ds(pl.multiple_of(ch * cw, cw), cw)
+    def ac(ch):
+        return pl.ds(pl.multiple_of(ch * ra_w, ra_w), ra_w)
+
+    def rc(ch):
+        return pl.ds(pl.multiple_of(ch * rs_w, rs_w), rs_w)
 
     def blocks(value):
         return value.reshape(NB, BLK, value.shape[1])
@@ -291,27 +410,29 @@
     scatter_y = Scatter(pc, party, side, rsys, rsyr, rsum)
 
     def embed(ch):
-        part[:, :, cols(ch)] = blocks(dot_nn(onehot[ALL], table[:, cols(ch)]).astype(BF16))
+        part[:, :, rc(ch)] = blocks(dot_nn(onehot[ALL], table[:, rc(ch)]).astype(BF16))
 
     def unpack_wqkv(s):
-        @pl.when(s < NCH)
-        def _():
-            slot = lax.rem(s, 2)
-            raw_load(s, slot).wait()
-
-            def body(i, _):
+        def piece(q):
+            p = s * (NW // NR) + q
+            slot = lax.rem(p, 2)
+            raw_load(p, slot).wait()
+
+            def body(i):
                 wstage[ALL] = wraw[slot, pl.ds(pl.multiple_of(i * QKV, QKV), QKV), :].astype(F32)
-                out_row = pl.multiple_of(s * cw + i * LANE, LANE)
+                out_row = pl.multiple_of(p * wq_w + i * LANE, LANE)
                 for j in range(6):
                     wq[pl.ds(out_row, LANE), j * LANE:(j + 1) * LANE] = wstage[pl.ds(j, LANE, stride=6), :].astype(BF16)
-                return 0
-            lax.fori_loop(0, raw_rows // QKV, body, 0)
-
-            @pl.when(s + 2 < NCH)
-            def _():
-                raw_load(s + 2, slot).start()
-
-    scatter.run(embed, unpack_wqkv)
+            loop(raw_rows // QKV, body)
+
+            @pl.when(p + 2 < NW)
+            def _():
+                raw_load(p + 2, slot).start()
+        loop(NW // NR, piece)
+
+    dy[pc.me] = dout[ALL]
+    gather_dy = Gather(pc, dy, agds, agdr)
+    scatter.run(embed, unpack_wqkv, gather_dy.start_y)
     e_norm, hat, inv = norm_forward(rsum[ALL], eg[ALL], eb[ALL])
     e_hat[ALL] = hat
     invs[0] = jnp.broadcast_to(inv, (BLK, LANE))
@@ -322,17 +443,14 @@
     invs[1] = jnp.broadcast_to(inv, (BLK, LANE))
     h1[pc.me] = n1_norm.astype(BF16)
 
-    gather = Gather(pc, h1, ags, agr, NCH)
+    gather = Gather(pc, h1, ags, agr)
     gather.start()
-    dy[pc.me] = dout[ALL]
     qkv_acc[ALL] = jnp.zeros_like(qkv_acc)
 
     def use_h1(ch):
-        qkv_acc[ALL] += dot_nn(rows(h1[:, :, cols(ch)]), wq[cols(ch), :])
-
-    gather.run(use_h1)
-    gather_dy = Gather(pc, dy, agds, agdr, NCH)
-    gather_dy.start()
+        qkv_acc[ALL] += dot_nn(rows(h1[:, :, ac(ch)]), wq[ac(ch), :])
+
+    gather.run(use_h1, gather_dy.start_z)
     out_h1 = pltpu.make_async_copy(h1, h1_o, osem.at[0])
     out_h1.start()
 
@@ -362,30 +480,18 @@
         ctx[:, h * LANE:(h + 1) * LANE] = dot_nn(p.astype(BF16), qkv[:, head_cols(2, h)]).astype(BF16)
 
     attend(0)
-    lax.fori_loop(0, NCH, lambda ch, u: (gather_dy.a(ch), u)[1], 0)
     attend(1)
+    loop(NA // 2, gather_dy.a)
     loads[1].wait()
 
     def dense(ch):
-        part[:, :, cols(ch)] = blocks(dot_nn(ctx[ALL], wd[:, cols(ch)]).astype(BF16))
-
-    dgelu[ALL] = jnp.zeros_like(dgelu)
-    loads[3].wait()
-
-    def use_dy(s):
-        @pl.when(s < NCH)
-        def _():
-            gather_dy.b(s)
-
-        @pl.when((s >= 1) & (s <= NCH))
-        def _():
-            gather_dy.c(s - 1)
-            dgelu[ALL] += dot_nt(rows(dy[:, :, cols(s - 1)]), w2[:, cols(s - 1)])
-
-    scatter.run(dense, use_dy)
-    gather_dy.finish()
-    out_dy = pltpu.make_async_copy(dy, dy_o, osem.at[1])
-    out_dy.start()
+        part[:, :, rc(ch)] = blocks(dot_nn(ctx[ALL], wd[:, rc(ch)]).astype(BF16))
+
+    def dy_rest():
+        loop(NA // 2, lambda ch: gather_dy.a(NA // 2 + ch))
+        loop(NA // 2, gather_dy.b)
+
+    scatter.run(dense, None, dy_rest)
     out_ctx = pltpu.make_async_copy(ctx, ctx_o, osem.at[2])
     out_ctx.start()
 
@@ -395,15 +501,29 @@
     n2_hat[ALL] = hat
     invs[2] = jnp.broadcast_to(inv, (BLK, LANE))
     h2[pc.me] = n2_norm.astype(BF16)
-    gather = Gather(pc, h2, ags, agr, NCH)
+    gather = Gather(pc, h2, ags, agr)
     gather.start()
     pre[ALL] = jnp.zeros_like(pre)
+    dgelu[ALL] = jnp.zeros_like(dgelu)
     loads[2].wait()
+    loads[3].wait()
 
     def use_h2(ch):
-        pre[ALL] += dot_nn(rows(h2[:, :, cols(ch)]), w1[cols(ch), :])
-
-    gather.run(use_h2)
+        pre[ALL] += dot_nn(rows(h2[:, :, ac(ch)]), w1[ac(ch), :])
+
+    def use_dy(s):
+        @pl.when(s < NA)
+        def _():
+            @pl.when(s < NA // 2)
+            def _():
+                gather_dy.b(NA // 2 + s)
+            gather_dy.c(s)
+            dgelu[ALL] += dot_nt(rows(dy[:, :, ac(s)]), w2[:, ac(s)])
+
+    gather.run(use_h2, None, use_dy)
+    gather_dy.finish()
+    out_dy = pltpu.make_async_copy(dy, dy_o, osem.at[1])
+    out_dy.start()
     out_h2 = pltpu.make_async_copy(h2, h2_o, osem.at[3])
     out_h2.start()
 
@@ -425,40 +545,32 @@
     out_dpre.start()
 
     def dh2(ch):
-        part[:, :, cols(ch)] = blocks(dot_nt(dpre[ALL], w1[cols(ch), :]).astype(BF16))
+        part[:, :, rc(ch)] = blocks(dot_nt(dpre[ALL], w1[rc(ch), :]).astype(BF16))
 
     def mlp(s):
-        @pl.when(s < NCH)
-        def _():
-            party[:, :, cols(s)] = blocks(dot_nn(gelu_bf[ALL], w2[:, cols(s)]).astype(BF16))
-
-    scatter.run(dh2, mlp)
+        party[:, :, rc(s)] = blocks(dot_nn(gelu_bf[ALL], w2[:, rc(s)]).astype(BF16))
+        scatter_y.s0(s)
+
+    scatter.run(dh2, mlp, lambda: loop(NR // 2, scatter_y.s1))
     dn, sg, sbv = norm_backward(rsum[ALL], n2_hat[ALL], invs[2, :, 0:1], g2[ALL])
     dr_val = dout[ALL].astype(F32) + dn
     dr_own[ALL] = dr_val
     dr[pc.me] = dr_val.astype(BF16)
-    st2[pc.me] = jnp.concatenate([sg, sbv], axis=0).astype(BF16)
-    gather = Gather(pc, dr, ags, agr, NCH)
+    stat[ALL] = jnp.zeros_like(stat)
+    stat[4:5, :] = sg
+    stat[5:6, :] = sbv
+    gather = Gather(pc, dr, ags, agr)
     gather.start()
-    gather_st = Gather(pc, st2, sts, strc, 1)
-    gather_st.start()
     d_ctx = qkv_acc.at[:, 0:256]
     d_ctx[ALL] = jnp.zeros((SEQ, 256), F32)
 
     def use_dr(ch):
-        d_ctx[ALL] += dot_nt(rows(dr[:, :, cols(ch)]), wd[:, cols(ch)])
-
-    def y_start(s):
-        @pl.when(s < NCH)
-        def _():
-            scatter_y.s0(s)
-
-    gather.run(use_dr, y_start)
+        d_ctx[ALL] += dot_nt(rows(dr[:, :, ac(ch)]), wd[:, ac(ch)])
+
+    gather.run(use_dr, lambda: loop(NR // 2, scatter_y.s2))
     out_dr = pltpu.make_async_copy(dr, dr_o, osem.at[6])
     out_dr.start()
-    gather_st.a(0)
-    lax.fori_loop(0, NCH, lambda ch, u: (scatter_y.s1(ch), u)[1], 0)
-    gather_st.b(0)
+    loop(NR // 4, lambda ch: scatter_y.s1(NR // 2 + ch))
 
     def attend_back(h):
         dc = d_ctx[:, h * LANE:(h + 1) * LANE].astype(BF16)
@@ -477,45 +589,45 @@
     attend_back(1)
     out_dqkv = pltpu.make_async_copy(dqkv, dqkv_o, osem.at[7])
     out_dqkv.start()
-    lax.fori_loop(0, NCH, lambda ch, u: (scatter_y.s2(ch), u)[1], 0)
-
-    gather_st.c(0)
-    gather_st.finish()
-
     def dh1(ch):
-        part[:, :, cols(ch)] = blocks(dot_nt(dqkv[ALL], wq[cols(ch), :]).astype(BF16))
-
-    scatter.run(dh1)
+        part[:, :, rc(ch)] = blocks(dot_nt(dqkv[ALL], wq[rc(ch), :]).astype(BF16))
+
+    def y_more():
+        loop(NR // 4, lambda ch: scatter_y.s1(NR * 3 // 4 + ch))
+        loop(NR // 4, lambda ch: scatter_y.s2(NR // 2 + ch))
+
+    scatter.run(dh1, None, y_more)
     dn, sg1, sb1 = norm_backward(rsum[ALL], n1_hat[ALL], invs[1, :, 0:1], g1[ALL])
     dxv, sg0, sb0 = norm_backward(dr_own[ALL] + dn, e_hat[ALL], invs[0, :, 0:1], eg[ALL])
     dx[pc.me] = dxv.astype(BF16)
-    st4[pc.me] = jnp.concatenate([sg0, sb0, sg1, sb1], axis=0).astype(BF16)
-    gather = Gather(pc, dx, ags, agr, NCH)
+    for i, row in enumerate((sg0, sb0, sg1, sb1)):
+        stat[i:i + 1, :] = row
+    sums = SmallSum(pc, stat, sv, sra, ssb, srb, srz, stot, sts, strc)
+    sums.t0()
+    gather = Gather(pc, dx, ags, agr)
     gather.start()
-    gather_st = Gather(pc, st4, sts, strc, 1)
-    gather_st.start()
-
-    lax.fori_loop(0, NCH, lambda ch, u: (scatter_y.s3(ch), u)[1], 0)
+
+    def sums_step(s):
+        for i, step in enumerate((sums.t1, sums.t2, sums.t3)):
+            pl.when(s == i)(step)
+
+        @pl.when(s < NA)
+        def _():
+            small_o[6:7, ac(s)] = jnp.sum(rows(dr[:, :, ac(s)]).astype(F32), axis=0, keepdims=True)
+            small_o[7:8, ac(s)] = jnp.sum(rows(dy[:, :, ac(s)]).astype(F32), axis=0, keepdims=True)
+
+    gather.run(None, lambda: loop(NR // 4, lambda ch: scatter_y.s2(NR * 3 // 4 + ch)), sums_step)
+    outs = [pltpu.make_async_copy(dx.at[block_of(t)], dx_o.at[t], osem.at[8]) for t in range(NB)]
+    for cp in outs:
+        cp.start()
+    loop(NR, scatter_y.s3)
     scatter_y.finish()
     y_o[ALL] = (r_one[ALL] + rsum[ALL] + bf2[ALL]).astype(BF16)
-    small_o[4:6, :] = jnp.sum(st2[ALL].astype(F32), axis=0)
-
-    def col_sums(s):
-        @pl.when(s < NCH)
-        def _():
-            small_o[6:7, cols(s)] = jnp.sum(rows(dr[:, :, cols(s)]).astype(F32), axis=0, keepdims=True)
-            small_o[7:8, cols(s)] = jnp.sum(rows(dy[:, :, cols(s)]).astype(F32), axis=0, keepdims=True)
-
-    gather.run(None, col_sums)
-    gather_st.a(0)
-    gather_st.b(0)
-    gather_st.c(0)
-    gather_st.finish()
-    small_o[0:4, :] = jnp.sum(st4[ALL].astype(F32), axis=0)
-    out_dx = pltpu.make_async_copy(dx, dx_o, osem.at[8])
-    out_dx.start()
-    for cp in (out_h1, out_dy, out_ctx, out_h2, out_gelu, out_dpre, out_dr, out_dqkv, out_dx):
+    sums.t4()
+    small_o[0:6, :] = stot[0:6, :]
+    for cp in (out_h1, out_dy, out_ctx, out_h2, out_gelu, out_dpre, out_dr, out_dqkv):
         cp.wait()
+    pltpu.make_async_copy(dx, dx_o, osem.at[8]).wait()
 
 
 def chain(ids, slopes, vecs, bqkv, bf1, dout, table, wqkv, wd, w1, w2):
@@ -533,18 +645,20 @@
                pltpu.VMEM((3, BLK, dim), BF16), pltpu.VMEM((3, BLK, dim), BF16)]
     row = pltpu.VMEM((BLK, dim), F32)
     dma = pltpu.SemaphoreType.DMA
-    scratch = [pltpu.VMEM((vocab_rows, dim), BF16), pltpu.VMEM((2, dim * 6 // NCH, LANE), BF16),
+    scratch = [pltpu.VMEM((vocab_rows, dim), BF16), pltpu.VMEM((2, dim * 6 // NW, LANE), BF16),
                pltpu.VMEM((dim, QKV), BF16), pltpu.VMEM(wd.shape, BF16), pltpu.VMEM(w1.shape, BF16),
                pltpu.VMEM(w2.shape, BF16), full, full, full, full, full,
-               pltpu.VMEM((NB, 2, dim), BF16), pltpu.VMEM((NB, 4, dim), BF16), full, full]
+               full, full]
     scratch += rs_bufs + rs_bufs
     scratch += [pltpu.VMEM((SEQ, vocab_rows), BF16), pltpu.VMEM((QKV, LANE), F32), pltpu.VMEM((SEQ, QKV), F32),
                 pltpu.VMEM((SEQ, QKV), BF16), pltpu.VMEM((2, SEQ, SEQ), F32), pltpu.VMEM((SEQ, 256), BF16),
                 pltpu.VMEM((SEQ, ff), F32), pltpu.VMEM((SEQ, ff), F32), pltpu.VMEM((SEQ, ff), BF16),
                 pltpu.VMEM((SEQ, ff), BF16), pltpu.VMEM((SEQ, QKV), BF16)]
     scratch += [row] * 7 + [pltpu.VMEM((3, BLK, LANE), F32)]
-    scratch += [dma((6,)), dma((9,)), dma((NCH, 9)), dma((NCH, 9)), dma((NCH, 9)), dma((NCH, 9)),
-                dma((NCH, 5)), dma((NCH, 5)), dma((NCH, 5)), dma((NCH, 5)), dma((1, 9)), dma((1, 9))]
+    half = pltpu.VMEM((8, dim // 2), BF16)
+    scratch += [pltpu.VMEM((8, dim), F32), pltpu.VMEM((8, dim), BF16), half, half, half,
+                pltpu.VMEM((4, 8, dim // 2), BF16), pltpu.VMEM((8, dim), F32)]
+    scratch += [dma((6,)), dma((9,))] + [dma((NA, 11)), dma((NA, 9))] * 2 + [dma((NR, 5))] * 4 + [dma((6,))] * 2
     return pl.pallas_call(
         chain_kernel, out_shape=out_shape,
         in_specs=[vmem, pl.BlockSpec(memory_space=pltpu.SMEM)] + [vmem] * 11 + [hbm] * 5,
@@ -577,19 +691,18 @@
                 w_fc1, b_fc1, w_fc2, b_fc2, d_out, slopes_all):
     dim = embed_table.shape[1]
     vocab_rows = embed_table.shape[0]
-    ids = token_ids.reshape(4, 2, 2, BLK).transpose(2, 1, 0, 3).reshape(SEQ, 1)
     vecs = [v.reshape(1, dim) for v in (emb_gain, emb_bias, ln1_gain, ln1_bias, ln2_gain, ln2_bias, b_dense, b_fc2)]
     wqkv = w_qkv.transpose(0, 2, 1, 3).reshape(dim * 6, LANE)
     (h1, h2, dy, dr, dx, ctx, gelu, dpre, dqkv, y, small, dbf1, dbqkv) = chain(
-        ids, slopes_all, vecs, b_qkv.transpose(1, 0, 2), b_fc1.reshape(1, -1), d_out.reshape(BLK, dim),
+        token_ids, slopes_all, vecs, b_qkv.transpose(1, 0, 2), b_fc1.reshape(1, -1), d_out.reshape(BLK, dim),
         embed_table, wqkv, w_dense, w_fc1, w_fc2)
     h1, h2, dy, dr, dx = (v.reshape(SEQ, dim) for v in (h1, h2, dy, dr, dx))
     d_w_qkv = qkv_grad(h1, dqkv).reshape(dim, 3, 2, LANE).transpose(0, 2, 1, 3)
     d_w_fc2 = dot_tn(gelu, dy).astype(BF16)
     d_w_fc1 = dot_tn(h2, dpre).astype(BF16)
     d_w_dense = dot_tn(ctx, dr).astype(BF16)
-    one_hot = (ids - lax.axis_index('tp') * vocab_rows == jnp.arange(vocab_rows)[None, :]).astype(BF16)
-    d_table = dot_tn(one_hot, dx)
+    one_hot = (token_ids - lax.axis_index('tp') * vocab_rows == jnp.arange(vocab_rows)[:, None]).astype(BF16)
+    d_table = dot_nn(one_hot, dx)
     return (y[None], d_table, small[0], small[1], small[2], small[3],
             d_w_qkv, dbqkv.transpose(1, 0, 2), d_w_dense, small[6], small[4], small[5],
             d_w_fc1, dbf1.reshape(-1), d_w_fc2, small[7])

time: 251 us -> 214 us (0.85)
  Pallas kernels: 222 us -> 188 us
    pallas_call x1, Pallas kernels: 212 us -> 179 us  [chain(): pl.pallas_call(chain_kernel, out_shape=out_shape, in_specs=[vmem, pl.Bloc...]
    dot_general x4 -> x3, matrix products: 22 us -> 15.5 us  [dot_tn(): lax.dot_general(a, b, (((0,), (0,)), ((), ())), preferred_element_type=F32)]
    dot_general x0 -> x1, matrix products: none -> 6.29 us  [dot_nn(): lax.dot_general(a, b, (((1,), (0,)), ((), ())), preferred_element_type=F32)]
where the time goes in v2:
time: 214 us; the launch traced here: 213 us
  Pallas kernels  188 us (88%)
  matrix products  21.8 us (10%)
  local copies, waits for them, and re-layouts  2.58 us (1%)
    pallas_call x1, Pallas kernels, chain(): pl.pallas_call(chain_kernel, out_shape=out_shape, in_specs=[vmem, pl.Bloc...  179 us
    dot_general x3, matrix products, dot_tn(): lax.dot_general(a, b, (((0,), (0,)), ((), ())), preferred_element_type=F32)  15.5 us
    pallas_call x1, Pallas kernels, qkv_grad(): pl.pallas_call(qkv_grad_kernel, out_shape=jax.ShapeDtypeStruct((dim * 6,...  9.2 us
    dot_general x1, matrix products, dot_nn(): lax.dot_general(a, b, (((1,), (0,)), ((), ())), preferred_element_type=F32)  6.29 us

profile of v2, /device:TPU:0, one launch (start us, length us, event | category | flops | bytes accessed | tf_op | source)
XLA Modules:
  0.0 213.2 jit_solution(15190569702514999051)
XLA Ops:
  0.7 178.9 %chain.1 = (bf16[16,16,4096]{2,1,0:T(8,128)(2,1)}, bf16[16,16,4096]{2,1,0:T(8,128)(2,1)}, bf16[16,16,4096]{2,1,0:T(8,128)(2,1)}, bf16[16,16,4096]{2,1,0:T(8,128)...) custom-call(s32[1,256]{1,0:T(1,128)} %ids.1, ...), custom_call_target="tpu_custom_call" | custom-call | tf_op jit(solution)/shard_map/chain/pallas_call | solution.py:662
  179.6 0.0 copy-start
  179.6 0.0 copy-start.2
  179.6 7.7 %convolution_convert_fusion = bf16[1024,4096]{1,0:T(8,128)(2,1)} fusion(bf16[256,1024]{1,0:T(8,128)(2,1)} %get-tuple-element.40, bf16[256,4096]{1,0:T(8,128)(2,1)} %bitcast.47), kind=kOutput, calls=%fused_computation | convolution fusion | flops 2151677952 | bytes 11010048 | tf_op jit(solution)/shard_map/dot_general | solution.py:58
  187.3 0.0 copy-done
  187.3 0.0 copy-done.2
  187.3 5.8 %convolution_convert_fusion.1 = bf16[4096,1024]{1,0:T(8,128)(2,1)} fusion(bf16[256,4096]{1,0:T(8,128)(2,1)S(1)} %bitcast.43, bf16[256,1024]{1,0:T(8,128)(2,1)S(1)} %copy-done.2), kind=kOutput, calls=%fused_computation.1 | convolution fusion | flops 2151677952 | bytes 11010048 | tf_op jit(solution)/shard_map/dot_general | solution.py:58
  193.1 0.0 copy-start.1
  193.1 0.0 copy-start.3
  193.1 9.2 %qkv_grad.1 = bf16[24576,128]{1,0:T(8,128)(2,1)} custom-call(bf16[256,4096]{1,0:T(8,128)(2,1)} %bitcast.46, bf16[256,768]{1,0:T(8,128)(2,1)} %get-tuple-element.33.dqkv), custom_call_target="tpu_custom_call" | custom-call | tf_op jit(solution)/shard_map/qkv_grad/pallas_call | solution.py:682
  202.3 0.0 copy-done.1
  202.3 0.0 copy-done.3
  202.3 0.0 copy-start.5
  202.3 0.0 copy-start.6
  202.3 2.1 convolution_convert_fusion.2
  204.4 0.0 copy-done.5
  204.4 0.7 fusion.2
  205.1 0.0 copy-done.6
  205.1 0.0 copy-start.4
  205.1 0.0 copy-start.8
  205.1 0.0 copy-start.7
  205.1 6.3 %fusion = f32[512,4096]{1,0:T(8,128)} fusion(bf16[256,4096]{1,0:T(8,128)(2,1)} %bitcast.45, s32[256]{0:T(256)S(1)} %bitcast.66), kind=kOutput, calls=%fused_computation.4 | convolution fusion | flops 1073872896 | bytes 10486784 | tf_op jit(solution)/shard_map/dot_general | solution.py:50
  211.4 0.0 copy-done.4
  211.4 0.7 copy.37
  212.1 0.0 copy-done.8
  212.1 0.6 copy.38
  212.6 0.0 copy-done.7
  212.6 0.6 copy.39
  (1 shorter events, 0.0 us)
Async XLA Ops:
  179.6 7.7 %copy-start = (bf16[16,16,4096]{2,1,0:T(8,128)(2,1)S(1)}, bf16[16,16,4096]{2,1,0:T(8,128)(2,1)}, u32[]{:S(2)}) copy-start(bf16[16,16,4096]{2,1,0:T(8,128)(2,1)} %get-tuple-element.37) | copy-start | bytes 6291460
  179.6 7.7 %copy-start.2 = (bf16[256,1024]{1,0:T(8,128)(2,1)S(1)}, bf16[256,1024]{1,0:T(8,128)(2,1)}, u32[]{:S(2)}) copy-start(bf16[256,1024]{1,0:T(8,128)(2,1)} %get-tuple-element.38) | copy-start | bytes 1572868
  193.1 9.2 %copy-start.1 = (bf16[16,16,4096]{2,1,0:T(8,128)(2,1)S(1)}, bf16[16,16,4096]{2,1,0:T(8,128)(2,1)}, u32[]{:S(2)}) copy-start(bf16[16,16,4096]{2,1,0:T(8,128)(2,1)} %get-tuple-element.36) | copy-start | bytes 6291460
  193.1 9.2 %copy-start.3 = (bf16[256,256]{1,0:T(8,128)(2,1)S(1)}, bf16[256,256]{1,0:T(8,128)(2,1)}, u32[]{:S(2)}) copy-start(bf16[256,256]{1,0:T(8,128)(2,1)} %get-tuple-element.35) | copy-start | bytes 393220
  202.3 2.1 copy-start.5
  202.3 2.8 %copy-start.6 = (s32[1,256]{1,0:T(1,128)S(1)}, s32[1,256]{1,0:T(1,128)}, u32[]{:S(2)}) copy-start(s32[1,256]{1,0:T(1,128)} %ids.1) | copy-start | bytes 3076
  205.1 6.3 %copy-start.4 = (bf16[16,4096]{1,0:T(8,128)(2,1)S(1)}, bf16[16,4096]{1,0:T(8,128)(2,1)}, u32[]{:S(2)}) copy-start(bf16[16,4096]{1,0:T(8,128)(2,1)} %get-tuple-element.29) | copy-start | bytes 393220
  205.1 7.0 %copy-start.8 = (f32[3,2,128]{2,1,0:T(2,128)S(1)}, f32[3,2,128]{2,1,0:T(2,128)}, u32[]{:S(2)}) copy-start(f32[3,2,128]{2,1,0:T(2,128)} %get-tuple-element.34) | copy-start | bytes 9220
  205.1 7.5 %copy-start.7 = (f32[1,1024]{1,0:T(1,128)S(1)}, f32[1,1024]{1,0:T(1,128)}, u32[]{:S(2)}) copy-start(f32[1,1024]{1,0:T(1,128)} %get-tuple-element.39) | copy-start | bytes 12292

commit v3 on v2

--- a/solution.py
+++ b/solution.py
@@ -669,21 +669,98 @@
     )(ids, slopes, *vecs, bqkv, bf1, dout, table, wqkv, wd, w1, w2)
 
 
-def qkv_grad_kernel(h1, dqkv, out, stage):
-    n = h1.shape[1]
-    for j in range(6):
-        stage[pl.ds(j, n, stride=6), :] = dot_tn(h1[ALL], dqkv[:, j * LANE:(j + 1) * LANE])
-    out[ALL] = stage[ALL].astype(BF16)
-
-
-def qkv_grad(h1, dqkv):
-    dim = h1.shape[1]
-    step = 512
+def grads_kernel(ids, gelu_h, dy_h, h2_h, dpre_h, h1_h, dqkv_h, ctx_h, dr_h, dx_h, y_h, small_h, dbf1_h, dbqkv_h,
+                 y_o, table_o, eg_o, eb_o, g1_o, b1_o, wqkv_o, bqkv_o, wd_o, bd_o, g2_o, b2_o, w1_o, bf1_o, w2_o, bf2_o,
+                 gelu, dy, h2, dpre, h1, dqkv, ctx, dr, dx, y, small, dbf1, dbqkv,
+                 w2, w1, wqkv, wd, table, stage, isem, osem):
+    pairs = ((gelu_h, gelu), (dy_h, dy), (h2_h, h2), (dpre_h, dpre), (h1_h, h1), (dqkv_h, dqkv), (ctx_h, ctx),
+             (dr_h, dr), (dx_h, dx), (y_h, y), (small_h, small), (dbf1_h, dbf1), (dbqkv_h, dbqkv))
+    loads = [pltpu.make_async_copy(src, dst, isem.at[i]) for i, (src, dst) in enumerate(pairs)]
+    for cp in loads:
+        cp.start()
+    pending = []
+
+    def tiles(count, src, dst, fn):
+        slot = len(pending)
+        n = src.shape[0] // count
+
+        def body(i):
+            tile = pl.ds(pl.multiple_of(i * n, n), n)
+            fn(i, tile)
+            pltpu.make_async_copy(src.at[tile], dst.at[tile], osem.at[slot]).start()
+        loop(count, body)
+        pending.append(pltpu.make_async_copy(src, dst, osem.at[slot]))
+
+    def ready(*which):
+        for i in which:
+            loads[i].wait()
+
+    def lane_tile(i, n):
+        return pl.ds(pl.multiple_of(i * n, n), n)
+
+    ready(0, 1)
+
+    def fc2(i, tile):
+        w2[tile, :] = dot_tn(gelu[:, tile], dy[ALL]).astype(BF16)
+    tiles(4, w2, w2_o, fc2)
+    ready(2, 3)
+
+    def fc1(i, tile):
+        w1[tile, :] = dot_tn(h2[:, tile], dpre[ALL]).astype(BF16)
+    tiles(8, w1, w1_o, fc1)
+    ready(8)
+    rows_here = table.shape[0]
+    local_ids = ids[ALL] - lax.axis_index('tp') * rows_here
+
+    def tab(i, tile):
+        n = rows_here // 4
+        hit = (local_ids == lax.broadcasted_iota(jnp.int32, (n, SEQ), 0) + i * n).astype(F32).astype(BF16)
+        table[tile, :] = dot_nn(hit, dx[ALL])
+    tiles(4, table, table_o, tab)
+    ready(4, 5)
+
+    def qkv(i, tile):
+        n = h1.shape[1] // 8
+        for j in range(6):
+            stage[pl.ds(j, n, stride=6), :] = dot_tn(h1[:, lane_tile(i, n)], dqkv[:, j * LANE:(j + 1) * LANE])
+        wqkv[tile, :] = stage[ALL].astype(BF16)
+    tiles(8, wqkv, wqkv_o, qkv)
+    ready(6, 7)
+
+    def dense(i, tile):
+        wd[tile, :] = dot_tn(ctx[:, tile], dr[ALL]).astype(BF16)
+    tiles(2, wd, wd_o, dense)
+    ready(9, 10, 11, 12)
+    rest = [(y, y_o), (dbf1, bf1_o), (dbqkv, bqkv_o)]
+    for i, out in enumerate((eg_o, eb_o, g1_o, b1_o, g2_o, b2_o, bd_o, bf2_o)):
+        rest.append((small.at[i:i + 1, :], out))
+    for src, dst in rest:
+        cp = pltpu.make_async_copy(src, dst, osem.at[len(pending)])
+        cp.start()
+        pending.append(cp)
+    for cp in pending:
+        cp.wait()
+
+
+def grads(ids, gelu, dy, h2, dpre, h1, dqkv, ctx, dr, dx, y, small, dbf1, dbqkv, vocab_rows):
+    dim, ff = dy.shape[1], gelu.shape[1]
+    ins = (gelu, dy, h2, dpre, h1, dqkv, ctx, dr, dx, y, small, dbf1, dbqkv)
+
+    def sds(*shape, dtype=F32):
+        return jax.ShapeDtypeStruct(shape, dtype)
+    row = sds(1, dim)
+    w2, w1, wqkv, wd = (sds(*shape, dtype=BF16) for shape in ((ff, dim), (dim, ff), (dim * 6, LANE), ctx.shape[1:] + (dim,)))
+    table = sds(vocab_rows, dim)
+    hbm = pl.BlockSpec(memory_space=pl.ANY)
+    out_shape = [sds(*y.shape, dtype=BF16), table, row, row, row, row, wqkv, sds(*dbqkv.shape), wd, row, row, row,
+                 w1, sds(1, ff), w2, row]
+    scratch = [pltpu.VMEM(v.shape, v.dtype) for v in ins + (w2, w1, wqkv, wd, table)]
+    scratch += [pltpu.VMEM((dim * 6 // 8, LANE), F32), pltpu.SemaphoreType.DMA((16,)), pltpu.SemaphoreType.DMA((16,))]
     return pl.pallas_call(
-        qkv_grad_kernel, out_shape=jax.ShapeDtypeStruct((dim * 6, LANE), BF16), grid=(dim // step,),
-        in_specs=[pl.BlockSpec((SEQ, step), lambda i: (0, i)), pl.BlockSpec((SEQ, QKV), lambda i: (0, 0))],
-        out_specs=pl.BlockSpec((step * 6, LANE), lambda i: (i, 0)),
-        scratch_shapes=[pltpu.VMEM((step * 6, LANE), F32)], name='qkv_grad')(h1, dqkv)
+        grads_kernel, out_shape=out_shape,
+        in_specs=[pl.BlockSpec(memory_space=pltpu.VMEM)] + [hbm] * len(ins), out_specs=[hbm] * 16,
+        scratch_shapes=scratch, name='grads',
+        compiler_params=pltpu.CompilerParams(vmem_limit_bytes=67043328))(ids, *ins)
 
 
 def device_step(token_ids, embed_table, emb_gain, emb_bias, ln1_gain, ln1_bias,
@@ -697,15 +774,13 @@
         token_ids, slopes_all, vecs, b_qkv.transpose(1, 0, 2), b_fc1.reshape(1, -1), d_out.reshape(BLK, dim),
         embed_table, wqkv, w_dense, w_fc1, w_fc2)
     h1, h2, dy, dr, dx = (v.reshape(SEQ, dim) for v in (h1, h2, dy, dr, dx))
-    d_w_qkv = qkv_grad(h1, dqkv).reshape(dim, 3, 2, LANE).transpose(0, 2, 1, 3)
-    d_w_fc2 = dot_tn(gelu, dy).astype(BF16)
-    d_w_fc1 = dot_tn(h2, dpre).astype(BF16)
-    d_w_dense = dot_tn(ctx, dr).astype(BF16)
-    one_hot = (token_ids - lax.axis_index('tp') * vocab_rows == jnp.arange(vocab_rows)[:, None]).astype(BF16)
-    d_table = dot_nn(one_hot, dx)
-    return (y[None], d_table, small[0], small[1], small[2], small[3],
-            d_w_qkv, dbqkv.transpose(1, 0, 2), d_w_dense, small[6], small[4], small[5],
-            d_w_fc1, dbf1.reshape(-1), d_w_fc2, small[7])
+    (y, d_table, d_eg, d_eb, d_g1, d_b1, d_w_qkv, d_b_qkv, d_wd, d_bd, d_g2, d_b2, d_w1, d_bf1, d_w2, d_bf2) = grads(
+        token_ids, gelu, dy, h2, dpre, h1, dqkv, ctx, dr, dx, y, small, dbf1, dbqkv, vocab_rows)
+    flat = [v.reshape(-1) for v in (d_eg, d_eb, d_g1, d_b1, d_bd, d_g2, d_b2, d_bf1, d_bf2)]
+    d_eg, d_eb, d_g1, d_b1, d_bd, d_g2, d_b2, d_bf1, d_bf2 = flat
+    return (y[None], d_table, d_eg, d_eb, d_g1, d_b1,
+            d_w_qkv.reshape(dim, 3, 2, LANE).transpose(0, 2, 1, 3), d_b_qkv.transpose(1, 0, 2), d_wd, d_bd, d_g2, d_b2,
+            d_w1, d_bf1, d_w2, d_bf2)
 
 
 def solution(mesh):

time: 214 us -> 199 us (0.930)
  matrix products: 21.8 us -> 0 us
  Pallas kernels: 188 us -> 198 us
  local copies, waits for them, and re-layouts: 2.58 us -> 0 us
    dot_general x4 -> x0, matrix products: 21.8 us -> none  [the longest x3 15.5 us: dot_tn(): lax.dot_general(a, b, (((0,), (0,)), ((), ())), preferred_element_type=F32)]
    pallas_call x1, Pallas kernels: 9.2 us -> 18.9 us  [grads(): pl.pallas_call(grads_kernel, out_shape=out_shape, in_specs=[pl.BlockSpec(...]
where the time goes in v3:
time: 199 us
  Pallas kernels  198 us (99%)
    pallas_call x1, Pallas kernels, chain(): pl.pallas_call(chain_kernel, out_shape=out_shape, in_specs=[vmem, pl.Bloc...  179 us
    pallas_call x1, Pallas kernels, grads(): pl.pallas_call(grads_kernel, out_shape=out_shape, in_specs=[pl.BlockSpec(...  18.9 us

profile of v3, /device:TPU:0, one launch (start us, length us, event | category | flops | bytes accessed | tf_op | source)
XLA Modules:
  0.0 198.5 jit_solution(17439057664368816397)
XLA Ops:
  0.7 179.0 %chain.1 = (bf16[16,16,4096]{2,1,0:T(8,128)(2,1)}, bf16[16,16,4096]{2,1,0:T(8,128)(2,1)}, bf16[16,16,4096]{2,1,0:T(8,128)(2,1)}, bf16[16,16,4096]{2,1,0:T(8,128)...) custom-call(s32[1,256]{1,0:T(1,128)} %ids.3, ...), custom_call_target="tpu_custom_call" | custom-call | tf_op jit(solution)/shard_map/chain/pallas_call | solution.py:662
  179.6 18.9 %grads.1 = (bf16[16,4096]{1,0:T(8,128)(2,1)}, f32[512,4096]{1,0:T(8,128)}, f32[1,4096]{1,0:T(1,128)}, f32[1,4096]{1,0:T(1,128)}, f32[1,4096]{1,0:T(1,128)}, /*in...) custom-call(s32[1,256]{1,0:T(1,128)} %ids.3, ...), custom_call_target="tpu_custom_call" | custom-call | tf_op jit(solution)/shard_map/grads/pallas_call | solution.py:759
